TPU v7x, 32 devices: a whole 2x2x4 slice. The times are simulated.
32 devices in a mesh: gx: 4 (over y, x), gy: 4 (over z), gz: 2 (over core).
Axes of the slice: x: 2, y: 2, z: 4, core: 2. Of those that a mesh axis runs over, the one named last changes fastest.
Arguments:
- estimate: float32 [16, 256, 512], P('gz', 'gx', 'gy'), may hold values from 0.25 to 4
- view_data: float32 [16, 256, 512], P('gz', 'gx', 'gy'), may hold values from 0.25 to 4
- psf_stack: float32 [6, 31, 31, 31], replicated, may hold values from 0.01 to 1.53, as said below
- view_index: int32 [1], replicated, may hold values from 0 to 5
Outputs:
- updated_estimate: float32 [16, 256, 512], P('gz', 'gx', 'gy')
- level_one: float32 [8, 128, 256], P('gz', 'gx', 'gy')
- level_two: float32 [4, 64, 128], P('gz', 'gx', 'gy')
- level_three: float32 [2, 32, 64], P('gz', 'gx', 'gy')
- level_four: float32 [1, 16, 32], P(None, 'gx', 'gy')
- level_five: float32 [1, 8, 16], replicated
Inputs may be any that keep to these rules, and one draw needn't show every extreme that they name: `psf_stack`: every entry of every view's point spread function is positive.
All inputs are finite; a program needn't handle non-finite values.
Results may differ from a plain program's by a relative error of at most 0.000075.
Values sent between devices are 32-bit elements; how exact they have to be, the bound alone decides.
A program may use at most 128 MiB of HBM per device.

v0:
```python
import functools
import math

import jax
import jax.numpy as jnp
import numpy as np
from jax import lax
from jax.experimental import pallas as pl
from jax.experimental.pallas import tpu as pltpu
from jax.sharding import PartitionSpec as P

MESH = pl.DeviceIdType.MESH
BF = jnp.bfloat16
F32 = jnp.float32
LANES = 128
EDGE = 16
TABLES = 11
DIRECTIONS = ((1, 0), (-1, 0), (0, 1), (0, -1), (1, 1), (-1, 1), (1, -1), (-1, -1))


def two_parts(matrix):
    matrix = np.asarray(matrix, np.float32)
    high = matrix.astype(BF)
    low = (matrix - high.astype(np.float32)).astype(BF)
    return high, low


def split(x):
    high = x.astype(BF)
    return high, (x - high.astype(F32)).astype(BF)


def dot(a, b):
    return jnp.dot(a, b, preferred_element_type=F32)


def tables(nx, ny, extent):
    radius = (extent - 1) // 2
    lx, ly = nx + 2 * EDGE, ny + 2 * EDGE
    nf = ly // 2 + 1
    freq_y = np.arange(nf)
    freq_x = np.arange(lx)

    def wave(k, n, length):
        return 2 * math.pi / length * np.mod(np.outer(k, n), length)

    pos = np.concatenate([EDGE + np.arange(ny), np.arange(EDGE), EDGE + ny + np.arange(EDGE)])
    fy = np.zeros((ny + LANES, 2 * LANES))
    angle = wave(pos, freq_y, ly)
    fy[: pos.size, :nf] = np.cos(angle)
    fy[: pos.size, LANES : LANES + nf] = -np.sin(angle)
    ky = np.zeros((LANES, 2 * LANES))
    angle = wave(np.arange(extent) - radius, freq_y, ly)
    ky[:extent, :nf] = np.cos(angle)
    ky[:extent, LANES : LANES + nf] = -np.sin(angle)
    iy = np.zeros((2 * LANES, ny))
    weight = np.full((nf, 1), 2.0)
    weight[0] = weight[-1] = 1.0
    angle = wave(freq_y, EDGE + np.arange(ny), ly)
    iy[:nf] = weight / ly * np.cos(angle)
    iy[LANES : LANES + nf] = -weight / ly * np.sin(angle)

    angle = wave(freq_x, np.arange(lx), lx)
    fx = np.block([[np.cos(angle), np.sin(angle)], [-np.sin(angle), np.cos(angle)]])
    angle = wave(EDGE + np.arange(nx), freq_x, lx)
    ix = np.block([[np.cos(angle), -np.sin(angle)], [np.sin(angle), np.cos(angle)]]) / lx
    kx = np.zeros((2 * lx, 2, extent + 1))
    angle = wave(freq_x, np.arange(extent) - radius, lx)
    kx[:lx, 0, :extent] = np.cos(angle)
    kx[:lx, 1, :extent] = np.sin(angle)
    kx[lx:, 0, :extent] = -np.sin(angle)
    kx[lx:, 1, :extent] = np.cos(angle)
    kx = kx.reshape(2 * lx, 2 * (extent + 1))

    fy_hi, fy_lo = two_parts(fy)
    ky_hi, ky_lo = two_parts(ky)
    iy_hi, iy_lo = two_parts(iy)
    fx_hi, fx_lo = two_parts(fx)
    ix_hi, ix_lo = two_parts(ix)
    kx_hi, kx_lo = two_parts(kx)

    py = np.zeros((ny, LANES))
    px = np.zeros((nx, nx))
    row, col = 0, 0
    places = []
    for level in range(1, 6):
        size = 2**level
        rows, cols = nx // size, ny // size
        places.append((row, rows, col, cols))
        for r in range(rows):
            px[row + r, r * size : (r + 1) * size] = 1.0 / size
        for c in range(cols):
            py[c * size : (c + 1) * size, col + c] = 1.0 / size
        row, col = row + rows, col + cols
    arrays = (
        fy_hi,
        fy_lo,
        np.concatenate([fx_hi, fx_lo], 0),
        ky_hi,
        ky_lo,
        np.concatenate([kx_hi, kx_hi, kx_lo], 1),
        np.concatenate([ix_hi, ix_lo], 0),
        iy_hi,
        iy_lo,
        py.astype(BF),
        px.astype(BF),
    )
    return arrays, tuple(places)


def kernel(
    sizes,
    places,
    index_ref, est_hbm, view_hbm, psf_hbm, *rest,
):
    count = TABLES
    tables_hbm, rest = rest[:count], rest[count:]
    body(
        sizes, places, index_ref, (est_hbm, psf_hbm, *tables_hbm, view_hbm), *rest
    )


def body(
    sizes,
    places,
    index_ref, operands,
    out_ref, one_ref, two_ref, three_ref, four_ref, five_ref,
    psf_pad, kd, k2, own, peer, mix, ratio,
    pack, xhalo, yhalo, share, share_in, tiles,
    in_sem, xs, xr, hs, hr, es, er, ps, pr, gs, gr,
    est_ref, psf, fy_hi, fy_lo, fx2, ky_hi, ky_lo, kx3, ix2, iy_hi, iy_lo, py, px, view_ref,
):
    gxn, gyn = sizes
    nz, nx, ny = est_ref.shape
    extent = psf.shape[1]
    pairs = nz // 2
    lx = nx + 2 * EDGE
    gx, gy, gz = lax.axis_index("gx"), lax.axis_index("gy"), lax.axis_index("gz")
    partner = {"gx": gx, "gy": gy, "gz": 1 - gz}
    chips = gxn * gyn

    resident = (
        est_ref, psf, fy_hi, fy_lo, fx2, ky_hi, ky_lo, kx3, ix2, iy_hi, iy_lo, py, px, view_ref
    )
    loads = [
        pltpu.make_async_copy(a, b, in_sem.at[i])
        for i, (a, b) in enumerate(zip(operands, resident))
    ]
    loads[0].start()

    def chip_at(offset):
        x = lax.rem(gx + offset // gyn, gxn)
        y = lax.rem(gy + lax.rem(offset, gyn), gyn)
        return {"gx": x, "gy": y, "gz": gz}

    barrier = pltpu.get_barrier_semaphore()
    pl.semaphore_signal(barrier, inc=1, device_id=partner, device_id_type=MESH)

    @pl.loop(1, chips)
    def _(offset):
        pl.semaphore_signal(barrier, inc=1, device_id=chip_at(offset), device_id_type=MESH)

    for load in loads[1:]:
        load.start()

    def exists(dx, dy):
        ok = None
        for c, n, d in ((gx, gxn, dx), (gy, gyn, dy)):
            if d > 0:
                t = c < n - 1
            elif d < 0:
                t = c > 0
            else:
                continue
            ok = t if ok is None else jnp.logical_and(ok, t)
        return ok

    def halo_parts(phase, field, dx, dy):
        if dy == 0:
            rows = slice(nx - EDGE, nx) if dx > 0 else slice(0, EDGE)
            return field.at[:, rows, :], xhalo.at[phase, 0 if dx > 0 else 1]
        side = 0 if dy > 0 else 1
        if dx == 0:
            return pack.at[phase, side], yhalo.at[phase, side, pl.ds(EDGE, nx), :]
        rows = pl.ds(nx - EDGE, EDGE) if dx > 0 else pl.ds(0, EDGE)
        to = pl.ds(0, EDGE) if dx > 0 else pl.ds(EDGE + nx, EDGE)
        return pack.at[phase, side, rows, :], yhalo.at[phase, side, to, :]

    def halo_copy(phase, field, d):
        dx, dy = DIRECTIONS[d]
        source, target = halo_parts(phase, field, dx, dy)
        return pltpu.make_async_remote_copy(
            src_ref=source,
            dst_ref=target,
            send_sem=hs.at[phase, d],
            recv_sem=hr.at[phase, d],
            device_id={"gx": gx + dx, "gy": gy + dy, "gz": gz},
            device_id_type=MESH,
        )

    def pair_copy(phase, field, d, q):
        source, target = halo_parts(phase, field, *DIRECTIONS[d])
        planes = pl.ds(2 * q, 2)
        rows = pl.ds(nx - EDGE, EDGE) if d == 0 else pl.ds(0, EDGE)
        return pltpu.make_async_remote_copy(
            src_ref=field.at[planes, rows, :],
            dst_ref=xhalo.at[phase, d, planes],
            send_sem=xs.at[phase, d, q],
            recv_sem=xr.at[phase, d, q],
            device_id={"gx": gx + DIRECTIONS[d][0], "gy": gy, "gz": gz},
            device_id_type=MESH,
        )

    def for_existing(towards, directions, act):
        for d in directions:
            dx, dy = DIRECTIONS[d]

            @pl.when(exists(dx, dy) if towards else exists(-dx, -dy))
            def _():
                act(d)

    def send_pair(phase, field, q):
        for_existing(True, (0, 1), lambda d: pair_copy(phase, field, d, q).start())

    def wait_pair(phase, field, q):
        for_existing(False, (0, 1), lambda d: pair_copy(phase, field, d, q).wait_recv())

    def do_pack(phase, field):
        lane = lax.broadcasted_iota(jnp.int32, (nx, LANES), 1) // EDGE
        last = jnp.zeros((nx, LANES), F32)
        first = jnp.zeros((nx, LANES), F32)
        for z in range(nz):
            plane = field[z]
            last = jnp.where(lane == z, pltpu.roll(plane, (EDGE * z + EDGE) % LANES, 1), last)
            first = jnp.where(lane == z, pltpu.roll(plane, EDGE * z, 1) if z else plane, first)
        pack[phase, 0] = last
        pack[phase, 1] = first

    def zero_missing(phase):
        for d, (dx, dy) in enumerate(DIRECTIONS):
            target = halo_parts(phase, est_ref, dx, dy)[1]

            @pl.when(jnp.logical_not(exists(-dx, -dy)))
            def _():
                target[...] = jnp.zeros(target.shape, F32)

    others = range(2, 8)

    def send_others(phase, field):
        for_existing(True, others, lambda d: halo_copy(phase, field, d).start())

    def wait_others(phase, field):
        for_existing(False, others, lambda d: halo_copy(phase, field, d).wait_recv())

    def wait_sends(phase, field):
        for_existing(True, others, lambda d: halo_copy(phase, field, d).wait_send())
        for q in range(pairs):
            for_existing(True, (0, 1), lambda d: pair_copy(phase, field, d, q).wait_send())
            swap_copy(phase, q).wait_send()

    def swap_copy(phase, q):
        planes = pl.ds(2 * q, 2)
        return pltpu.make_async_remote_copy(
            src_ref=own.at[phase, planes],
            dst_ref=peer.at[phase, planes],
            send_sem=es.at[phase, q],
            recv_sem=er.at[phase, q],
            device_id=partner,
            device_id_type=MESH,
        )

    def forward(phase, field, q):
        lane = lax.broadcasted_iota(jnp.int32, (lx, LANES), 1)
        full = []
        for z in (2 * q, 2 * q + 1):
            rows = jnp.concatenate([xhalo[phase, 0, z], field[z], xhalo[phase, 1, z]], axis=0)
            left, right = yhalo[phase, 0], yhalo[phase, 1]
            if z:
                left = pltpu.roll(left, LANES - EDGE * z, 1)
            if z != 1:
                right = pltpu.roll(right, (EDGE - EDGE * z) % LANES, 1)
            side = jnp.where(lane < EDGE, left, jnp.where(lane < 2 * EDGE, right, 0.0))
            full.append(jnp.concatenate([rows, side], axis=1))
        hi, lo = split(jnp.concatenate(full, axis=0))
        x1 = dot(hi, fy_hi[...]) + dot(lo, fy_hi[...]) + dot(hi, fy_lo[...])
        stacked = [
            jnp.concatenate(
                [x1[k * lx : (k + 1) * lx, :LANES], x1[k * lx : (k + 1) * lx, LANES:]], axis=0
            )
            for k in range(2)
        ]
        hi, lo = split(jnp.concatenate(stacked, axis=1))
        both = dot(fx2[...], hi)
        x2 = both[: 2 * lx] + both[2 * lx :] + dot(fx2[pl.ds(0, 2 * lx), :], lo)
        own[phase, 2 * q] = x2[:, :LANES]
        own[phase, 2 * q + 1] = x2[:, LANES:]
        swap_copy(phase, q).start()

    def mix_planes(source, phase, base, conj, add, chosen):
        @pl.loop(0, lx // 8)
        def _(s):
            re = pl.ds(pl.multiple_of(s * 8, 8), 8)
            im = pl.ds(pl.multiple_of(lx + s * 8, 8), 8)
            vr = [source[phase, j, re, :] for j in range(nz)]
            vi = [source[phase, j, im, :] for j in range(nz)]
            kr, ki = {}, {}
            reach = [(j - i if conj else i - j) for i in chosen for j in range(nz)]
            for d in sorted(set(reach)):
                kr[d] = k2[base + d, re, :]
                ki[d] = k2[base + d, im, :]
            ks = {d: kr[d] - ki[d] if conj else kr[d] + ki[d] for d in kr}
            vs = [r + i for r, i in zip(vr, vi)]
            for i in chosen:
                a = b = c = None
                for j in range(nz):
                    d = j - i if conj else i - j
                    rr, ii, ss = kr[d] * vr[j], ki[d] * vi[j], ks[d] * vs[j]
                    a = rr if a is None else a + rr
                    b = ii if b is None else b + ii
                    c = ss if c is None else c + ss
                yr = a + b if conj else a - b
                yi = c - a + b if conj else c - a - b
                mix[i, re, :] = mix[i, re, :] + yr if add else yr
                mix[i, im, :] = mix[i, im, :] + yi if add else yi

    def inverse(planes, write, after):
        for z in planes:
            y = jnp.concatenate([mix[z], mix[z + 1]], axis=1)
            hi, lo = split(y)
            both = dot(ix2[...], hi)
            g = both[: 2 * nx] + both[2 * nx :] + dot(ix2[pl.ds(0, 2 * nx), :], lo)
            for k in range(2):
                part = g[:, k * LANES : (k + 1) * LANES]
                rows = jnp.concatenate([part[:nx], part[nx:]], axis=1)
                hi, lo = split(rows)
                write(
                    z + k,
                    dot(hi, iy_hi[...]) + dot(lo, iy_hi[...]) + dot(hi, iy_lo[...]),
                )
            after(z // 2)

    def convolve(phase, field, conj, groups, write, after):
        wait_others(phase, field)
        for q in range(pairs):
            wait_pair(phase, field, q)
            forward(phase, field, q)
        sign = 1 - 2 * gz if conj else 2 * gz - 1
        middle = (extent - 1) // 2
        mix_planes(own, phase, middle, conj, False, range(nz))
        for q in range(pairs):
            swap_copy(phase, q).wait_recv()
        size = nz // groups
        for n in range(groups):
            planes = range(n * size, (n + 1) * size)
            mix_planes(peer, phase, middle + sign * nz, conj, True, planes)
            inverse(planes[::2], write, after)

    zero_missing(0)
    loads[0].wait()
    do_pack(0, est_ref)
    pl.semaphore_wait(barrier, chips)
    for q in range(pairs):
        send_pair(0, est_ref, q)
    send_others(0, est_ref)
    zero_missing(1)

    for load in loads[1:]:
        load.wait()
    chosen = psf[index_ref[0]]
    total = jnp.sum(chosen, axis=0)
    total = jnp.sum(jnp.sum(total, axis=1, keepdims=True), axis=0, keepdims=True)
    psf_pad[...] = jnp.zeros(psf_pad.shape, F32)
    psf_pad[pl.ds(0, extent), pl.ds(0, extent), pl.ds(0, extent)] = chosen * (1.0 / total)[None]
    wide = extent + 1

    @pl.loop(0, wide // 4)
    def _(q):
        block = psf_pad[pl.ds(q * 4, 4)].reshape(4 * wide, LANES)
        hi, lo = split(block)
        x1 = dot(hi, ky_hi[...]) + dot(lo, ky_hi[...]) + dot(hi, ky_lo[...])
        hi, lo = split(x1)
        hi = hi.reshape(4, wide, 2 * LANES)
        lo = lo.reshape(4, wide, 2 * LANES)
        for n, part in enumerate((hi, lo, hi)):
            kd[pl.ds(q * 4, 4), pl.ds(2 * n * wide, wide), :] = part[:, :, :LANES]
            kd[pl.ds(q * 4, 4), pl.ds(2 * n * wide + wide, wide), :] = part[:, :, LANES:]

    @pl.loop(0, wide // 4)
    def _(q):
        for h in range(2):
            n = q * 4 + 2 * h
            pair = jnp.concatenate([kd[n], kd[n + 1]], axis=1)
            spectrum = dot(kx3[...], pair)
            k2[n] = spectrum[:, :LANES]
            k2[n + 1] = spectrum[:, LANES:]

    def write_ratio(z, blurred):
        ratio[z] = view_ref[z] / blurred

    convolve(0, est_ref, False, 2, write_ratio, lambda q: send_pair(1, ratio, q))

    do_pack(1, ratio)
    send_others(1, ratio)

    def write_update(z, correction):
        out_ref[z] = est_ref[z] * correction

    convolve(1, ratio, True, 1, write_update, lambda q: None)

    halves = [(out_ref[2 * i] + out_ref[2 * i + 1]) * 0.5 for i in range(nz // 2)]
    quarters = [(halves[2 * i] + halves[2 * i + 1]) * 0.5 for i in range(nz // 4)]
    eighth = (quarters[0] + quarters[1]) * 0.5

    def pooled(plane):
        hi, lo = split(plane)
        t = dot(hi, py[...]) + dot(lo, py[...])
        hi, lo = split(t)
        return dot(px[...], hi) + dot(px[...], lo)

    r4, c4 = places[3][0], places[3][2]
    last = pooled(eighth)
    share[0] = last[r4 : r4 + 8]
    share_copy = pltpu.make_async_remote_copy(
        src_ref=share.at[0], dst_ref=share_in, send_sem=ps, recv_sem=pr,
        device_id=partner, device_id_type=MESH,
    )
    share_copy.start()
    row, rows, col, cols = places[2]
    three_ref[0] = last[row : row + rows, col : col + cols]
    row, rows, col, cols = places[1]
    for i, plane in enumerate(quarters):
        two_ref[i] = pooled(plane)[row : row + rows, col : col + cols]
    share_copy.wait()
    both = (share[0] + share_in[...]) * 0.5
    four_ref[0] = both[: places[3][1], c4 : c4 + places[3][3]]
    row, rows, col, cols = places[4]
    row = row - r4
    r = lax.broadcasted_iota(jnp.int32, both.shape, 0)
    c = lax.broadcasted_iota(jnp.int32, both.shape, 1)
    inside = (r >= row) & (r < row + rows) & (c >= col) & (c < col + cols)
    mine = jnp.where(inside, both, 0.0)
    height = tiles.shape[1]
    if height > 8:
        mine = jnp.concatenate([mine, jnp.zeros((height - 8, LANES), F32)], axis=0)
    mine = pltpu.roll(mine, lax.rem(gy * cols + LANES - col, LANES), 1)
    mine = pltpu.roll(mine, lax.rem(gx * rows + height - row, height), 0)
    tiles[0] = mine

    def tile_copy(offset):
        return pltpu.make_async_remote_copy(
            src_ref=tiles.at[0], dst_ref=tiles.at[offset],
            send_sem=gs.at[offset], recv_sem=gr.at[offset],
            device_id=chip_at(offset), device_id_type=MESH,
        )

    @pl.loop(1, chips)
    def _(offset):
        tile_copy(offset).start()

    row, rows, col, cols = places[0]
    for i, plane in enumerate(halves):
        one_ref[i] = pooled(plane)[row : row + rows, col : col + cols]
    for phase, field in ((0, est_ref), (1, ratio)):
        wait_sends(phase, field)

    @pl.loop(1, chips)
    def _(offset):
        tile_copy(offset).wait()

    five = tiles[0]
    for offset in range(1, chips):
        five = five + tiles[offset]
    five_ref[0] = five[: five_ref.shape[1], : five_ref.shape[2]]


def write_out(*refs):
    sems = refs[12]
    copies = [pltpu.make_async_copy(refs[i], refs[6 + i], sems.at[i]) for i in range(6)]
    for copy in copies:
        copy.start()
    for copy in copies:
        copy.wait()


def local(sizes, estimate, view_data, psf_stack, view_index):
    gxn, gyn = sizes
    nz, nx, ny = estimate.shape
    views, extent = psf_stack.shape[:2]
    arrays, places = tables(nx, ny, extent)
    lx = nx + 2 * EDGE
    wide = extent + 1
    chips = gxn * gyn
    vmem = pl.BlockSpec(memory_space=pltpu.VMEM)
    hbm = pl.BlockSpec(memory_space=pltpu.HBM)

    def shape(*dims):
        return jax.ShapeDtypeStruct(dims, F32)

    rows5, cols5 = places[4][1] * gxn, places[4][3] * gyn
    dma = pltpu.SemaphoreType.DMA
    shapes = (
        shape(nz, nx, ny),
        shape(nz // 2, nx // 2, ny // 2),
        shape(nz // 4, nx // 4, ny // 4),
        shape(nz // 8, nx // 8, ny // 8),
        shape(1, nx // 16, ny // 16),
        shape(1, rows5, cols5),
    )
    results = pl.pallas_call(
        functools.partial(kernel, sizes, places),
        out_shape=shapes,
        in_specs=[pl.BlockSpec(memory_space=pltpu.SMEM)] + [hbm] * (len(arrays) + 3),
        out_specs=(vmem,) * 6,
        scratch_shapes=[
            pltpu.VMEM((wide, wide, LANES), F32),
            pltpu.VMEM((wide, 6 * wide, LANES), BF),
            pltpu.VMEM((wide, 2 * lx, LANES), F32),
            pltpu.VMEM((2, nz, 2 * lx, LANES), F32),
            pltpu.VMEM((2, nz, 2 * lx, LANES), F32),
            pltpu.VMEM((nz, 2 * lx, LANES), F32),
            pltpu.VMEM((nz, nx, ny), F32),
            pltpu.VMEM((2, 2, nx, LANES), F32),
            pltpu.VMEM((2, 2, nz, EDGE, ny), F32),
            pltpu.VMEM((2, 2, lx, LANES), F32),
            pltpu.VMEM((1, 8, LANES), F32),
            pltpu.VMEM((8, LANES), F32),
            pltpu.VMEM((chips, max(8, rows5), LANES), F32),
            dma((len(arrays) + 3,)),
            dma((2, 2, nz // 2)),
            dma((2, 2, nz // 2)),
            dma((2, 8)),
            dma((2, 8)),
            dma((2, nz // 2)),
            dma((2, nz // 2)),
            dma,
            dma,
            dma((chips,)),
            dma((chips,)),
            *[pltpu.VMEM(a.shape, a.dtype) for a in (estimate, psf_stack, *arrays, view_data)],
        ],
        compiler_params=pltpu.CompilerParams(
            collective_id=0, has_side_effects=True, vmem_limit_bytes=67043328 - 450000
        ),
        name="deconvolve",
    )(view_index, estimate, view_data, psf_stack, *[jnp.asarray(a) for a in arrays])
    return pl.pallas_call(
        write_out,
        out_shape=shapes,
        in_specs=[vmem] * 6,
        out_specs=(hbm,) * 6,
        scratch_shapes=[dma((6,))],
        name="write_out",
    )(*results)


def solution(mesh):
    return jax.shard_map(
        functools.partial(local, (mesh.shape["gx"], mesh.shape["gy"])),
        mesh=mesh,
        in_specs=(P("gz", "gx", "gy"), P("gz", "gx", "gy"), P(), P()),
        out_specs=(
            P("gz", "gx", "gy"),
            P("gz", "gx", "gy"),
            P("gz", "gx", "gy"),
            P("gz", "gx", "gy"),
            P(None, "gx", "gy"),
            P(),
        ),
        check_vma=False,
    )
```

profile of v0, /device:TPU:0, one launch (start us, length us, event | category | flops | bytes accessed | tf_op | source)
XLA Modules:
  0.0 37.8 jit_solution(13812907665553103026)
XLA Ops:
  1.3 34.7 %deconvolve.1 = (f32[8,64,128]{2,1,0:T(8,128)}, f32[4,32,64]{2,1,0:T(8,128)}, f32[2,16,32]{2,1,0:T(8,128)}, f32[1,8,16]{2,1,0:T(8,128)}, f32[1,4,8]{2,1,0:T(4,128)}, /*index=5*/f32[1,8,16]{2,1,0:T(8,128)}) custom-call(s32[1]{0:T(128)S(6)} %copy.21.index_ref, f32[8,64,128]{2,1,0:T(8,128)} %est_hbm.1, f32[8,64,128]{2,1,0:T(8,128)} %view_hbm.1, ...), custom_call_target="tpu_custom_call" | custom-call | tf_op jit(solution)/shard_map/deconvolve/pallas_call | solution.py:509
  36.0 1.8 %write_out.1 = (f32[8,64,128]{2,1,0:T(8,128)}, f32[4,32,64]{2,1,0:T(8,128)}, f32[2,16,32]{2,1,0:T(8,128)}, f32[1,8,16]{2,1,0:T(8,128)}, f32[1,4,8]{2,1,0:T(4,128)}, /*index=5*/f32[1,8,16]{2,1,0:T(8,128)}) custom-call(f32[8,64,128]{2,1,0:T(8,128)} %get-tuple-element.12.refs_0_, f32[4,32,64]{2,1,0:T(8,128)} %get-tuple-element.13.refs_1_, ...), custom_call_target="tpu_custom_call" | custom-call | tf_op jit(solution)/shard_map/write_out/pallas_call | solution.py:546
where the time goes:
time: 37.9 us; the launch traced here: 37.8 us
  Pallas kernels  36.5 us (96%)
  between operations  1.29 us (3%)
    pallas_call x1, Pallas kernels, local(): pl.pallas_call(functools.partial(kernel, sizes, places), out_shape=shapes...  34.7 us
    pallas_call x1, Pallas kernels, local(): pl.pallas_call(write_out, out_shape=shapes, in_specs=[vmem] * 6, out_spec...  1.78 us

commit v1 on v0

v1 whole, which is shorter than its diff:
```python
import functools
import math

import jax
import jax.numpy as jnp
import numpy as np
from jax import lax
from jax.experimental import pallas as pl
from jax.experimental.pallas import tpu as pltpu
from jax.sharding import PartitionSpec as P

MESH = pl.DeviceIdType.MESH
NS = jax.named_scope
BF = jnp.bfloat16
F32 = jnp.float32
LANES = 128
EDGE = 16
GROUP = 8
CORNERS = ((1, 1), (-1, 1), (1, -1), (-1, -1))
SIDES_X = ((1, 0), (-1, 0))
SIDES_Y = ((0, 1), (0, -1))


def two_parts(matrix):
    matrix = np.asarray(matrix, np.float32)
    high = matrix.astype(BF)
    low = (matrix - high.astype(np.float32)).astype(BF)
    return high, low


def split(x):
    high = x.astype(BF)
    return high, (x - high.astype(F32)).astype(BF)


def dot(a, b):
    return jnp.dot(a, b, preferred_element_type=F32)


def tables(nx, ny, extent):
    radius = (extent - 1) // 2
    lx, ly = nx + 2 * EDGE, ny + 2 * EDGE
    nf = ly // 2 + 1
    wide = extent + 1
    freq_y = np.arange(nf)
    freq_x = np.arange(lx)

    def wave(k, n, length):
        return 2 * math.pi / length * np.mod(np.outer(k, n), length)

    pos = np.concatenate([EDGE + np.arange(ny), np.arange(EDGE), EDGE + ny + np.arange(EDGE)])
    fy = np.zeros((ny + 2 * EDGE, 2 * LANES))
    angle = wave(pos, freq_y, ly)
    fy[:, :nf] = np.cos(angle)
    fy[:, LANES : LANES + nf] = -np.sin(angle)
    ky = np.zeros((wide, 2 * LANES))
    angle = wave(np.arange(extent) - radius, freq_y, ly)
    ky[:extent, :nf] = np.cos(angle)
    ky[:extent, LANES : LANES + nf] = -np.sin(angle)
    iy = np.zeros((2 * LANES, ny))
    weight = np.full((nf, 1), 2.0)
    weight[0] = weight[-1] = 1.0
    angle = wave(freq_y, EDGE + np.arange(ny), ly)
    iy[:nf] = weight / ly * np.cos(angle)
    iy[LANES : LANES + nf] = -weight / ly * np.sin(angle)

    angle = wave(freq_x, np.arange(lx), lx)
    fx = np.block([[np.cos(angle), np.sin(angle)], [-np.sin(angle), np.cos(angle)]])
    angle = wave(EDGE + np.arange(nx), freq_x, lx)
    ix = np.block([[np.cos(angle), -np.sin(angle)], [np.sin(angle), np.cos(angle)]]) / lx
    kx = np.zeros((2 * lx, 2, wide))
    angle = wave(freq_x, np.arange(extent) - radius, lx)
    kx[:lx, 0, :extent] = np.cos(angle)
    kx[:lx, 1, :extent] = np.sin(angle)
    kx[lx:, 0, :extent] = -np.sin(angle)
    kx[lx:, 1, :extent] = np.cos(angle)
    kx = kx.reshape(2 * lx, 2 * wide)

    fy_hi, fy_lo = two_parts(fy)
    ky_hi, ky_lo = two_parts(ky)
    iy_hi, iy_lo = two_parts(iy)
    fx_hi, fx_lo = two_parts(fx)
    ix_hi, ix_lo = two_parts(ix)
    kx_hi, kx_lo = two_parts(kx)

    py = np.zeros((ny, LANES))
    px = np.zeros((nx, nx))
    row, col = 0, 0
    places = []
    for level in range(1, 5):
        size = 2**level
        rows, cols = nx // size, ny // size
        places.append((row, rows, col, cols))
        for r in range(rows):
            px[row + r, r * size : (r + 1) * size] = 1.0 / size
        for c in range(cols):
            py[c * size : (c + 1) * size, col + c] = 1.0 / size
        row, col = row + rows, col + cols

    blank = np.zeros((LANES - 3 * wide, 2 * LANES), BF)
    side_hi, side_lo = fy_hi[ny:], fy_lo[ny:]
    named = {
        "fya": np.concatenate([fy_hi[:ny], fy_hi[:ny]], 0),
        "fyb": np.concatenate([fy_lo[:ny], side_hi, side_hi, side_lo, blank], 0),
        "fx2": np.concatenate([fx_hi, fx_lo], 0),
        "ky3": np.concatenate([ky_hi, ky_hi, ky_lo, blank], 0),
        "kx3": np.concatenate([kx_hi, kx_hi, kx_lo], 1),
        "ix2": np.concatenate([ix_hi, ix_lo], 0),
        "iyh": iy_hi,
        "iyl": iy_lo,
        "py": py.astype(BF),
        "px": px.astype(BF),
    }
    stacked, where, row = [], {}, 0
    for name, a in named.items():
        rows, cols = a.shape
        where[name] = (row, rows, cols)
        full = np.zeros((rows, 2 * LANES), BF)
        full[:, :cols] = a
        stacked.append(full)
        row += rows
    return np.concatenate(stacked, 0), where, tuple(places)


def kernel(
    sizes, where, places,
    index_hbm, est_hbm, view_hbm, psf_hbm, table_hbm,
    out_ref, one_ref, two_ref, three_ref, four_ref, five_ref,
    index_ref, est_ref, view_ref, psf, table,
    psf_pad, k2, own, peer, mix, ratio,
    pack, xhalo, yhalo, share, share_in, place5, mine, tiles, ruler,
    in_sem, hs, hr, es, er, ps, pr, gs, gr,
):
    gxn, gyn = sizes
    nz, nx, ny = est_ref.shape
    extent = psf.shape[1]
    wide = extent + 1
    pairs = nz // 2
    lx = nx + 2 * EDGE
    nf = (ny + 2 * EDGE) // 2 + 1
    third = lx // 3
    lp = 2 * third
    half = (nf + 1) // 2
    middle = (extent - 1) // 2
    gx, gy, gz = lax.axis_index("gx"), lax.axis_index("gy"), lax.axis_index("gz")
    partner = {"gx": gx, "gy": gy, "gz": 1 - gz}
    chips = gxn * gyn
    everyone = 2 * chips

    def tab(name, first=0, count=None):
        row, rows, cols = where[name]
        return table[pl.ds(row + first, rows if count is None else count), pl.ds(0, cols)]

    load_est, load_index, load_psf, load_table, load_view = [
        pltpu.make_async_copy(a, b, in_sem.at[i])
        for i, (a, b) in enumerate(
            (
                (est_hbm, est_ref),
                (index_hbm, index_ref),
                (psf_hbm, psf),
                (table_hbm, table),
                (view_hbm, view_ref),
            )
        )
    ]
    load_est.start()

    def device_at(offset):
        chip = offset // 2
        x = lax.rem(gx + chip // gyn, gxn)
        y = lax.rem(gy + lax.rem(chip, gyn), gyn)
        return {"gx": x, "gy": y, "gz": lax.rem(gz + lax.rem(offset, 2), 2)}

    barrier = pltpu.get_barrier_semaphore()

    @pl.loop(1, everyone)
    def _(offset):
        pl.semaphore_signal(barrier, inc=1, device_id=device_at(offset), device_id_type=MESH)

    load_psf.start()
    load_index.start()
    load_table.start()
    load_view.start()

    def exists(dx, dy):
        ok = None
        for c, n, d in ((gx, gxn, dx), (gy, gyn, dy)):
            if d > 0:
                t = c < n - 1
            elif d < 0:
                t = c > 0
            else:
                continue
            ok = t if ok is None else jnp.logical_and(ok, t)
        return ok

    def halo_copy(phase, field, dx, dy, planes=None):
        if dy == 0:
            rows = slice(nx - EDGE, nx) if dx > 0 else slice(0, EDGE)
            source = field.at[planes, rows, :]
            target = xhalo.at[phase, 0 if dx > 0 else 1, planes]
        else:
            side = 0 if dy > 0 else 1
            if dx == 0:
                source, target = pack.at[phase, side], yhalo.at[phase, side, pl.ds(EDGE, nx), :]
            else:
                rows = pl.ds(nx - EDGE, EDGE) if dx > 0 else pl.ds(0, EDGE)
                to = pl.ds(0, EDGE) if dx > 0 else pl.ds(EDGE + nx, EDGE)
                source, target = pack.at[phase, side, rows, :], yhalo.at[phase, side, to, :]
        return pltpu.make_async_remote_copy(
            src_ref=source,
            dst_ref=target,
            send_sem=hs.at[phase],
            recv_sem=hr.at[phase],
            device_id={"gx": gx + dx, "gy": gy + dy, "gz": gz},
            device_id_type=MESH,
        )

    def send_halo(phase, field, directions, planes=None):
        for dx, dy in directions:

            @pl.when(exists(dx, dy))
            def _():
                halo_copy(phase, field, dx, dy, planes).start()

    beside_x = (gx > 0).astype(jnp.int32) + (gx < gxn - 1).astype(jnp.int32)
    beside_y = (gy > 0).astype(jnp.int32) + (gy < gyn - 1).astype(jnp.int32)

    def settle(sem):
        for a in range(3):
            for b in range(3):
                rows = nz * EDGE * a + nx * b + EDGE * a * b
                if rows:

                    @pl.when(jnp.logical_and(beside_x == a, beside_y == b))
                    def _():
                        part = ruler.at[pl.ds(0, rows)]
                        pltpu.make_async_copy(part, part, sem).wait()

    def add_to_pack(phase, z, plane, first):
        lane = lax.broadcasted_iota(jnp.int32, (nx, LANES), 1) // EDGE
        for side, shift in ((0, EDGE * z + EDGE), (1, EDGE * z)):
            moved = pltpu.roll(plane, shift % LANES, 1) if shift % LANES else plane
            kept = 0.0 if first else pack[phase, side]
            pack[phase, side] = jnp.where(lane == z, moved, kept)

    def zero_missing(phase):
        for dx, dy in SIDES_X + SIDES_Y + CORNERS:
            if dy == 0:
                target = xhalo.at[phase, 0 if dx > 0 else 1]
            else:
                side = 0 if dy > 0 else 1
                first, count = {0: (EDGE, nx), 1: (0, EDGE), -1: (EDGE + nx, EDGE)}[dx]
                target = yhalo.at[phase, side, pl.ds(first, count), :]

            @pl.when(jnp.logical_not(exists(-dx, -dy)))
            def _():
                target[...] = jnp.zeros(target.shape, F32)

    def swap_copy(phase, first, count):
        planes = pl.ds(first, count)
        return pltpu.make_async_remote_copy(
            src_ref=own.at[phase, planes],
            dst_ref=peer.at[phase, planes],
            send_sem=es.at[phase],
            recv_sem=er.at[phase],
            device_id=partner,
            device_id_type=MESH,
        )

    def fold(x):
        lane = lax.broadcasted_iota(jnp.int32, (lp, LANES), 1)
        rest = x[lp:lx]
        beside = jnp.concatenate(
            [pltpu.roll(rest, nf, 1), pltpu.roll(rest, nf - half, 1)], axis=0
        )
        return jnp.where(lane < nf, x[:lp], beside)

    def unfold(x):
        lane = lax.broadcasted_iota(jnp.int32, (third, LANES), 1)
        low = pltpu.roll(x[:third], LANES - nf, 1)
        high = pltpu.roll(x[third:lp], LANES - (nf - half), 1)
        return jnp.concatenate([x[:lp], jnp.where(lane < half, low, high)], axis=0)

    def forward(phase, field, q):
        lane = lax.broadcasted_iota(jnp.int32, (lx, LANES), 1)
        rows, sides = [], []
        for z in (2 * q, 2 * q + 1):
            rows.append(xhalo[phase, 0, z])
            rows.append(field[z])
            rows.append(xhalo[phase, 1, z])
            left, right = yhalo[phase, 0], yhalo[phase, 1]
            if z:
                left = pltpu.roll(left, LANES - EDGE * z, 1)
            if z != 1:
                right = pltpu.roll(right, (EDGE - EDGE * z) % LANES, 1)
            side = jnp.where(lane < EDGE, left, jnp.where(lane < 2 * EDGE, right, 0.0))
            high = side.astype(BF).astype(F32)
            low = side - high
            sides.append(
                (high + pltpu.roll(low, 2 * EDGE, 1) + pltpu.roll(high, 4 * EDGE, 1)).astype(BF)
            )
        hi, lo = split(jnp.concatenate(rows, axis=0))
        x1 = dot(jnp.concatenate([hi, lo], axis=1), tab("fya")) + dot(
            jnp.concatenate([hi, jnp.concatenate(sides, axis=0)], axis=1), tab("fyb")
        )
        stacked = [
            jnp.concatenate(
                [x1[k * lx : (k + 1) * lx, :LANES], x1[k * lx : (k + 1) * lx, LANES:]], axis=0
            )
            for k in range(2)
        ]
        hi, lo = split(jnp.concatenate(stacked, axis=1))
        both = dot(tab("fx2"), hi)
        x2 = both[: 2 * lx] + both[2 * lx :] + dot(tab("fx2", 0, 2 * lx), lo)
        for k in range(2):
            part = x2[:, k * LANES : (k + 1) * LANES]
            own[phase, 2 * q + k, pl.ds(0, lp), :] = fold(part[:lx])
            own[phase, 2 * q + k, pl.ds(lp, lp), :] = fold(part[lx:])

    def mix_planes(source, phase, base, conj, add, chosen):
        @pl.loop(0, lp // 8)
        def _(s):
            re = pl.ds(pl.multiple_of(s * 8, 8), 8)
            im = pl.ds(pl.multiple_of(lp + s * 8, 8), 8)
            vr = [source[phase, j, re, :] for j in range(nz)]
            vi = [source[phase, j, im, :] for j in range(nz)]
            kr, ki = {}, {}
            reach = [(j - i if conj else i - j) for i in chosen for j in range(nz)]
            for d in sorted(set(reach)):
                kr[d] = k2[base + d, re, :]
                ki[d] = k2[base + d, im, :]
            ks = {d: kr[d] - ki[d] if conj else kr[d] + ki[d] for d in kr}
            vs = [r + i for r, i in zip(vr, vi)]
            for i in chosen:
                a = b = c = None
                for j in range(nz):
                    d = j - i if conj else i - j
                    rr, ii, ss = kr[d] * vr[j], ki[d] * vi[j], ks[d] * vs[j]
                    a = rr if a is None else a + rr
                    b = ii if b is None else b + ii
                    c = ss if c is None else c + ss
                yr = a + b if conj else a - b
                yi = c - a + b if conj else c - a - b
                mix[i, re, :] = mix[i, re, :] + yr if add else yr
                mix[i, im, :] = mix[i, im, :] + yi if add else yi

    def inverse(planes, write):
        for z in planes:
            y = jnp.concatenate(
                [
                    jnp.concatenate([unfold(mix[w, pl.ds(0, lp)]), unfold(mix[w, pl.ds(lp, lp)])], 0)
                    for w in (z, z + 1)
                ],
                axis=1,
            )
            hi, lo = split(y)
            both = dot(tab("ix2"), hi)
            g = both[: 2 * nx] + both[2 * nx :] + dot(tab("ix2", 0, 2 * nx), lo)
            for k in range(2):
                part = g[:, k * LANES : (k + 1) * LANES]
                rows = jnp.concatenate([part[:nx], part[nx:]], axis=1)
                hi, lo = split(rows)
                write(z + k, dot(hi, tab("iyh")) + dot(lo, tab("iyh")) + dot(hi, tab("iyl")))

    def prepare(first):
        block = psf_pad[pl.ds(first, GROUP)].reshape(GROUP * wide, LANES)
        high = block.astype(BF).astype(F32)
        low = block - high
        x1 = dot(
            (high + pltpu.roll(low, wide, 1) + pltpu.roll(high, 2 * wide, 1)).astype(BF),
            tab("ky3"),
        )
        hi, lo = split(x1)
        hi = hi.reshape(GROUP, wide, 2 * LANES)
        lo = lo.reshape(GROUP, wide, 2 * LANES)
        for h in range(GROUP // 2):
            columns = []
            for n in (2 * h, 2 * h + 1):
                parts = []
                for part in (hi[n], lo[n], hi[n]):
                    parts.append(part[:, :LANES])
                    parts.append(part[:, LANES:])
                columns.append(jnp.concatenate(parts, axis=0))
            spectrum = dot(tab("kx3"), jnp.concatenate(columns, axis=1))
            for n in range(2):
                part = spectrum[:, n * LANES : (n + 1) * LANES]
                k2[first + 2 * h + n, pl.ds(0, lp), :] = fold(part[:lx])
                k2[first + 2 * h + n, pl.ds(lp, lp), :] = fold(part[lx:])

    def convolve(phase, field, conj, groups, write, after):
        with NS(f"wait_halo{phase}"):
            settle(hr.at[phase])
        count = nz // 2
        for n in range(2):
            with NS(f"forward{phase}_{n}"):
                for q in range(n * pairs // 2, (n + 1) * pairs // 2):
                    forward(phase, field, q)
                swap_copy(phase, n * count, count).start()
        sign = 1 - 2 * gz if conj else 2 * gz - 1
        with NS(f"mixown{phase}"):
            mix_planes(own, phase, middle, conj, False, range(nz))
        if phase == 0:
            with NS("prepare2"):
                prepare(3 * GROUP * gz)
        with NS(f"waitswap{phase}"):
            pltpu.make_async_copy(own.at[phase], peer.at[phase], er.at[phase]).wait()
        size = nz // groups
        for n in range(groups):
            planes = range(n * size, (n + 1) * size)
            with NS(f"mixpeer{phase}_{n}"):
                mix_planes(peer, phase, middle + sign * nz, conj, True, planes)
            with NS(f"inverse{phase}_{n}"):
                inverse(planes[::2], write)
                after(planes)

    with NS("zero"):
        zero_missing(0)
        zero_missing(1)
    with NS("wait_est"):
        load_est.wait()
    with NS("pack0"):
        for z in range(nz):
            add_to_pack(0, z, est_ref[z], z == 0)
    with NS("barrier"):
        pl.semaphore_wait(barrier, everyone - 1)
    with NS("send0"):
        send_halo(0, est_ref, CORNERS)
        send_halo(0, est_ref, SIDES_X, pl.ds(0, nz))
        send_halo(0, est_ref, SIDES_Y)

    with NS("wait_loads"):
        load_index.wait()
        load_psf.wait()
        load_table.wait()
        load_view.wait()
    with NS("psf_prep"):
        chosen = psf[index_ref[0]]
        total = jnp.sum(chosen, axis=0)
        total = jnp.sum(jnp.sum(total, axis=1, keepdims=True), axis=0, keepdims=True)
        psf_pad[...] = jnp.zeros(psf_pad.shape, F32)
        psf_pad[pl.ds(0, extent), pl.ds(0, extent), pl.ds(0, extent)] = (
            chosen * (1.0 / total)[None]
        )

    with NS("prepare1"):

        @pl.loop(1, 3)
        def _(g):
            prepare(g * GROUP)

    def write_ratio(z, blurred):
        value = view_ref[z] / blurred
        ratio[z] = value
        add_to_pack(1, z, value, z == 0)

    def after_ratio(planes):
        if planes[-1] == nz - 1:
            send_halo(1, ratio, CORNERS)
        send_halo(1, ratio, SIDES_X, pl.ds(planes[0], len(planes)))
        if planes[-1] == nz - 1:
            send_halo(1, ratio, SIDES_Y)

    convolve(0, est_ref, False, 2, write_ratio, after_ratio)

    with NS("prepare3"):
        prepare(3 * GROUP * (1 - gz))
        cols5 = four_ref.shape[2] // 2
        i = lax.broadcasted_iota(jnp.int32, (LANES, LANES), 0)
        j = lax.broadcasted_iota(jnp.int32, (LANES, LANES), 1)
        target = i // (ny // cols5) + gy * cols5
        place5[...] = jnp.where(j == target, 1.0 / (nz * 2 * 32 * 32), 0.0).astype(BF)

    def write_update(z, correction):
        out_ref[z] = est_ref[z] * correction

    convolve(1, ratio, True, 1, write_update, lambda planes: None)

    with NS("five_send"):
        rows5 = four_ref.shape[1] // 2
        total = out_ref[0]
        for z in range(1, nz):
            total = total + out_ref[z]
        summed = jnp.sum(total.reshape(rows5, nx // rows5, ny), axis=1)
        hi, lo = split(summed)
        mine[...] = dot(hi, place5[...]) + dot(lo, place5[...])

        def slot(x, y, z):
            return (x * gyn + y) * 2 + z

        def tile_copy(offset):
            return pltpu.make_async_remote_copy(
                src_ref=mine,
                dst_ref=tiles.at[slot(gx, gy, gz)],
                send_sem=gs,
                recv_sem=gr,
                device_id=device_at(offset),
                device_id_type=MESH,
            )

        @pl.loop(1, everyone)
        def _(offset):
            tile_copy(offset).start()

        tiles[slot(gx, gy, gz)] = mine[...]

    def pooled(plane):
        hi, lo = split(plane)
        t = dot(hi, tab("py")) + dot(lo, tab("py"))
        hi, lo = split(t)
        return dot(tab("px"), hi) + dot(tab("px"), lo)

    with NS("pyramid"):
        halves = [(out_ref[2 * i] + out_ref[2 * i + 1]) * 0.5 for i in range(nz // 2)]
        quarters = [(halves[2 * i] + halves[2 * i + 1]) * 0.5 for i in range(nz // 4)]
        eighth = (quarters[0] + quarters[1]) * 0.5
        r4, c4 = places[3][0], places[3][2]
        last = pooled(eighth)
        share[0] = last[r4 : r4 + 8]
        share_copy = pltpu.make_async_remote_copy(
            src_ref=share.at[0], dst_ref=share_in, send_sem=ps, recv_sem=pr,
            device_id=partner, device_id_type=MESH,
        )
        share_copy.start()
        row, rows, col, cols = places[2]
        three_ref[0] = last[row : row + rows, col : col + cols]
        row, rows, col, cols = places[1]
        for i, plane in enumerate(quarters):
            two_ref[i] = pooled(plane)[row : row + rows, col : col + cols]
        row, rows, col, cols = places[0]
        for i, plane in enumerate(halves):
            one_ref[i] = pooled(plane)[row : row + rows, col : col + cols]
    with NS("share"):
        share_copy.wait()
        both = (share[0] + share_in[...]) * 0.5
        four_ref[0] = both[: places[3][1], c4 : c4 + places[3][3]]
    with NS("settle"):
        for phase in range(2):
            settle(hs.at[phase])
            pltpu.make_async_copy(own.at[phase], peer.at[phase], es.at[phase]).wait()
    with NS("wait_tiles"):
        others = tiles.at[pl.ds(0, everyone - 1)]
        pltpu.make_async_copy(others, others, gs).wait()
        pltpu.make_async_copy(others, others, gr).wait()
    with NS("five"):
        for x in range(gxn):
            five = tiles[slot(x, 0, 0)]
            for n in range(1, 2 * gyn):
                five = five + tiles[slot(x, 0, 0) + n]
            five_ref[0, pl.ds(x * rows5, rows5), :] = five[:, : five_ref.shape[2]]


def write_out(*refs):
    sems = refs[12]
    copies = [pltpu.make_async_copy(refs[i], refs[6 + i], sems.at[i]) for i in range(6)]
    for copy in copies:
        copy.start()
    for copy in copies:
        copy.wait()


def local(sizes, estimate, view_data, psf_stack, view_index):
    gxn, gyn = sizes
    nz, nx, ny = estimate.shape
    extent = psf_stack.shape[1]
    table, where, places = tables(nx, ny, extent)
    lx = nx + 2 * EDGE
    lp = 2 * (lx // 3)
    wide = extent + 1
    everyone = 2 * gxn * gyn
    vmem = pl.BlockSpec(memory_space=pltpu.VMEM)
    hbm = pl.BlockSpec(memory_space=pltpu.HBM)
    rows5, cols5 = nx // 32, ny // 32
    dma = pltpu.SemaphoreType.DMA
    shapes = (
        (nz, nx, ny),
        (nz // 2, nx // 2, ny // 2),
        (nz // 4, nx // 4, ny // 4),
        (nz // 8, nx // 8, ny // 8),
        (1, nx // 16, ny // 16),
        (1, rows5 * gxn, cols5 * gyn),
    )
    results = pl.pallas_call(
        functools.partial(kernel, sizes, where, places),
        out_shape=tuple(pltpu.VMEM(s, F32) for s in shapes),
        in_specs=[hbm] * 5,
        out_specs=(vmem,) * 6,
        scratch_shapes=[
            pltpu.SMEM(view_index.shape, view_index.dtype),
            pltpu.VMEM(estimate.shape, F32),
            pltpu.VMEM(view_data.shape, F32),
            pltpu.VMEM(psf_stack.shape, F32),
            pltpu.VMEM(table.shape, BF),
            pltpu.VMEM((wide, wide, LANES), F32),
            pltpu.VMEM((wide, 2 * lp, LANES), F32),
            pltpu.VMEM((2, nz, 2 * lp, LANES), F32),
            pltpu.VMEM((2, nz, 2 * lp, LANES), F32),
            pltpu.VMEM((nz, 2 * lp, LANES), F32),
            pltpu.VMEM((nz, nx, ny), F32),
            pltpu.VMEM((2, 2, nx, LANES), F32),
            pltpu.VMEM((2, 2, nz, EDGE, ny), F32),
            pltpu.VMEM((2, 2, lx, LANES), F32),
            pltpu.VMEM((1, 8, LANES), F32),
            pltpu.VMEM((8, LANES), F32),
            pltpu.VMEM((LANES, LANES), BF),
            pltpu.VMEM((rows5, LANES), F32),
            pltpu.VMEM((everyone, rows5, LANES), F32),
            pltpu.VMEM((2 * nz * EDGE + 2 * nx + 4 * EDGE, LANES), F32),
            dma((5,)),
            dma((2,)),
            dma((2,)),
            dma((2,)),
            dma((2,)),
            dma,
            dma,
            dma,
            dma,
        ],
        compiler_params=pltpu.CompilerParams(
            collective_id=0, has_side_effects=True, vmem_limit_bytes=48 * 1024 * 1024
        ),
        name="deconvolve",
    )(
        view_index,
        *[
            pltpu.with_memory_space_constraint(a, pltpu.HBM)
            for a in (estimate, view_data, psf_stack, jnp.asarray(table))
        ],
    )
    return pl.pallas_call(
        write_out,
        out_shape=tuple(jax.ShapeDtypeStruct(s, F32) for s in shapes),
        in_specs=[vmem] * 6,
        out_specs=(hbm,) * 6,
        scratch_shapes=[dma((6,))],
        name="write_out",
    )(*[pltpu.with_memory_space_constraint(r, pltpu.VMEM) for r in results])


def solution(mesh):
    return jax.shard_map(
        functools.partial(local, (mesh.shape["gx"], mesh.shape["gy"])),
        mesh=mesh,
        in_specs=(P("gz", "gx", "gy"), P("gz", "gx", "gy"), P(), P()),
        out_specs=(
            P("gz", "gx", "gy"),
            P("gz", "gx", "gy"),
            P("gz", "gx", "gy"),
            P("gz", "gx", "gy"),
            P(None, "gx", "gy"),
            P(),
        ),
        check_vma=False,
    )
```

time: 37.9 us -> 33.3 us (0.88)
  Pallas kernels: 36.5 us -> 31.9 us
    pallas_call x2, Pallas kernels: 36.5 us -> 31.9 us  [the longest x1 31.1 us: local(): pl.pallas_call(functools.partial(kernel, sizes, where, places), out_shape...]
where the time goes in v1:
time: 33.3 us; the launch traced here: 33.2 us
  Pallas kernels  31.9 us (96%)
  between operations  1.29 us (4%)
    pallas_call x1, Pallas kernels, local(): pl.pallas_call(functools.partial(kernel, sizes, where, places), out_shape...  31.1 us
    pallas_call x1, Pallas kernels, local(): pl.pallas_call(write_out, out_shape=tuple((jax.ShapeDtypeStruct(s, F32) f...  0.78 us

profile of v1, /device:TPU:0, one launch (start us, length us, event | category | flops | bytes accessed | tf_op | source)
XLA Modules:
  0.0 33.2 jit_solution(9936987622040843755)
XLA Ops:
  1.3 31.1 %deconvolve.1 = (f32[8,64,128]{2,1,0:T(8,128)S(1)}, f32[4,32,64]{2,1,0:T(8,128)S(1)}, f32[2,16,32]{2,1,0:T(8,128)S(1)}, f32[1,8,16]{2,1,0:T(8,128)S(1)}, f32[1,4...) custom-call(s32[1]{0:T(128)S(6)} %copy.11.index_hbm, f32[8,64,128]{2,1,0:T(8,128)} %est_hbm.1, f32[8,64,128]{2,1,0:T(8,128)} %view_hbm.1, ...), custom_call_target="tpu_custom_call" | custom-call | tf_op jit(solution)/shard_map/deconvolve/pallas_call | solution.py:583
  32.4 0.8 %write_out.1 = (f32[8,64,128]{2,1,0:T(8,128)}, f32[4,32,64]{2,1,0:T(8,128)}, f32[2,16,32]{2,1,0:T(8,128)}, f32[1,8,16]{2,1,0:T(8,128)}, f32[1,4,8]{2,1,0:T(4,128)}, /*index=5*/f32[1,8,16]{2,1,0:T(8,128)}) custom-call(f32[8,64,128]{2,1,0:T(8,128)S(1)} %get-tuple-element.12.refs_0_, f32[4,32,64]{2,1,0:T(8,128)S(1)} %get-tuple-element.13.refs_1_, ...), custom_call_target="tpu_custom_call" | custom-call | tf_op jit(solution)/shard_map/write_out/pallas_call | solution.py:630

commit v2 on v1

--- a/solution.py
+++ b/solution.py
@@ -97,17 +97,21 @@
             py[c * size : (c + 1) * size, col + c] = 1.0 / size
         row, col = row + rows, col + cols
 
+    inner = np.concatenate([EDGE + np.arange(nx), lx + EDGE + np.arange(nx)])
+    outer = np.setdiff1d(np.arange(2 * lx), inner)
     blank = np.zeros((LANES - 3 * wide, 2 * LANES), BF)
     side_hi, side_lo = fy_hi[ny:], fy_lo[ny:]
     named = {
         "fya": np.concatenate([fy_hi[:ny], fy_hi[:ny]], 0),
         "fyb": np.concatenate([fy_lo[:ny], side_hi, side_hi, side_lo, blank], 0),
-        "fx2": np.concatenate([fx_hi, fx_lo], 0),
+        "fxa": np.concatenate([fx_hi[:, inner], fx_hi[:, inner]], 1),
+        "fxb": fx_lo[:, inner],
+        "fxh": np.concatenate([fx_hi[:, outer], fx_hi[:, outer], fx_lo[:, outer]], 1),
         "ky3": np.concatenate([ky_hi, ky_hi, ky_lo, blank], 0),
         "kx3": np.concatenate([kx_hi, kx_hi, kx_lo], 1),
         "ix2": np.concatenate([ix_hi, ix_lo], 0),
-        "iyh": iy_hi,
-        "iyl": iy_lo,
+        "iy2": np.concatenate([iy_hi, iy_lo], 1),
+        "iy1": iy_hi,
         "py": py.astype(BF),
         "px": px.astype(BF),
     }
@@ -129,7 +133,7 @@
     index_ref, est_ref, view_ref, psf, table,
     psf_pad, k2, own, peer, mix, ratio,
     pack, xhalo, yhalo, share, share_in, place5, mine, tiles, ruler,
-    in_sem, hs, hr, es, er, ps, pr, gs, gr,
+    in_sem, hs, hx, hy, es, er, ps, pr, gs, gr,
 ):
     gxn, gyn = sizes
     nz, nx, ny = est_ref.shape
@@ -165,18 +169,33 @@
     ]
     load_est.start()
 
-    def device_at(offset):
-        chip = offset // 2
-        x = lax.rem(gx + chip // gyn, gxn)
-        y = lax.rem(gy + lax.rem(chip, gyn), gyn)
-        return {"gx": x, "gy": y, "gz": lax.rem(gz + lax.rem(offset, 2), 2)}
+    def for_others(act):
+        zs = (gz, 1 - gz)
+
+        def column(x, ys, skip):
+            for b, y in ys:
+                for c in range(2):
+                    if not (skip and b == 0 and c == 0):
+                        act({"gx": x, "gy": y, "gz": zs[c]})
+
+        order = sorted(range(gyn), key=lambda b: -min(b, gyn - b))
+        ys = [(b, lax.rem(gy + b, gyn)) for b in order]
+        if gxn <= 4:
+            for a in (*range(1, gxn), 0):
+                column(lax.rem(gx + a, gxn), ys, a == 0)
+        else:
+
+            @pl.loop(1, gxn)
+            def _(a):
+                column(lax.rem(gx + a, gxn), ys, False)
+
+            column(gx, ys, True)
+
+    def signal(device):
+        pl.semaphore_signal(barrier, inc=1, device_id=device, device_id_type=MESH)
 
     barrier = pltpu.get_barrier_semaphore()
-
-    @pl.loop(1, everyone)
-    def _(offset):
-        pl.semaphore_signal(barrier, inc=1, device_id=device_at(offset), device_id_type=MESH)
-
+    for_others(signal)
     load_psf.start()
     load_index.start()
     load_table.start()
@@ -211,25 +230,34 @@
             src_ref=source,
             dst_ref=target,
             send_sem=hs.at[phase],
-            recv_sem=hr.at[phase],
+            recv_sem=(hx if dx else hy).at[phase],
             device_id={"gx": gx + dx, "gy": gy + dy, "gz": gz},
             device_id_type=MESH,
         )
 
     def send_halo(phase, field, directions, planes=None):
-        for dx, dy in directions:
-
-            @pl.when(exists(dx, dy))
+        def send(dx, dy, condition=True):
+            @pl.when(jnp.logical_and(exists(dx, dy), condition))
             def _():
                 halo_copy(phase, field, dx, dy, planes).start()
 
+        odd = lax.rem(gx, 2) == 1
+        for dx, dy in directions:
+            if dx:
+                send(dx, dy, odd if dx > 0 else jnp.logical_not(odd))
+        for dx, dy in directions:
+            if dx:
+                send(dx, dy, odd if dx < 0 else jnp.logical_not(odd))
+            else:
+                send(dx, dy)
+
     beside_x = (gx > 0).astype(jnp.int32) + (gx < gxn - 1).astype(jnp.int32)
     beside_y = (gy > 0).astype(jnp.int32) + (gy < gyn - 1).astype(jnp.int32)
 
-    def settle(sem):
+    def settle(sem, along_x=True, along_y=True):
         for a in range(3):
             for b in range(3):
-                rows = nz * EDGE * a + nx * b + EDGE * a * b
+                rows = (nz * EDGE * a + EDGE * a * b) * along_x + nx * b * along_y
                 if rows:
 
                     @pl.when(jnp.logical_and(beside_x == a, beside_y == b))
@@ -237,12 +265,15 @@
                         part = ruler.at[pl.ds(0, rows)]
                         pltpu.make_async_copy(part, part, sem).wait()
 
-    def add_to_pack(phase, z, plane, first):
+    def add_to_pack(phase, field, planes):
         lane = lax.broadcasted_iota(jnp.int32, (nx, LANES), 1) // EDGE
-        for side, shift in ((0, EDGE * z + EDGE), (1, EDGE * z)):
-            moved = pltpu.roll(plane, shift % LANES, 1) if shift % LANES else plane
-            kept = 0.0 if first else pack[phase, side]
-            pack[phase, side] = jnp.where(lane == z, moved, kept)
+        for side in range(2):
+            kept = pack[phase, side] if planes[0] else jnp.zeros((nx, LANES), F32)
+            for z in planes:
+                shift = (EDGE * z + EDGE * (1 - side)) % LANES
+                moved = pltpu.roll(field[z], shift, 1) if shift else field[z]
+                kept = jnp.where(lane == z, moved, kept)
+            pack[phase, side] = kept
 
     def zero_missing(phase):
         for dx, dy in SIDES_X + SIDES_Y + CORNERS:
@@ -282,41 +313,55 @@
         high = pltpu.roll(x[third:lp], LANES - (nf - half), 1)
         return jnp.concatenate([x[:lp], jnp.where(lane < half, low, high)], axis=0)
 
-    def forward(phase, field, q):
-        lane = lax.broadcasted_iota(jnp.int32, (lx, LANES), 1)
-        rows, sides = [], []
-        for z in (2 * q, 2 * q + 1):
-            rows.append(xhalo[phase, 0, z])
-            rows.append(field[z])
-            rows.append(xhalo[phase, 1, z])
-            left, right = yhalo[phase, 0], yhalo[phase, 1]
-            if z:
-                left = pltpu.roll(left, LANES - EDGE * z, 1)
-            if z != 1:
-                right = pltpu.roll(right, (EDGE - EDGE * z) % LANES, 1)
-            side = jnp.where(lane < EDGE, left, jnp.where(lane < 2 * EDGE, right, 0.0))
-            high = side.astype(BF).astype(F32)
-            low = side - high
-            sides.append(
-                (high + pltpu.roll(low, 2 * EDGE, 1) + pltpu.roll(high, 4 * EDGE, 1)).astype(BF)
-            )
-        hi, lo = split(jnp.concatenate(rows, axis=0))
+    def beside(phase, z, first, count):
+        lane = lax.broadcasted_iota(jnp.int32, (count, LANES), 1)
+        left, right = (yhalo[phase, side, pl.ds(first, count), :] for side in range(2))
+        if z:
+            left = pltpu.roll(left, LANES - EDGE * z, 1)
+        if z != 1:
+            right = pltpu.roll(right, (EDGE - EDGE * z) % LANES, 1)
+        side = jnp.where(lane < EDGE, left, jnp.where(lane < 2 * EDGE, right, 0.0))
+        high = side.astype(BF).astype(F32)
+        low = side - high
+        return (high + pltpu.roll(low, 2 * EDGE, 1) + pltpu.roll(high, 4 * EDGE, 1)).astype(BF)
+
+    def along_y(rows, sides):
+        count = len(rows)
+        hi, lo = split(jnp.concatenate([jnp.concatenate(r, axis=0) for r in rows], axis=0))
+        side = jnp.concatenate([jnp.concatenate(r, axis=0) for r in sides], axis=0)
         x1 = dot(jnp.concatenate([hi, lo], axis=1), tab("fya")) + dot(
-            jnp.concatenate([hi, jnp.concatenate(sides, axis=0)], axis=1), tab("fyb")
-        )
+            jnp.concatenate([hi, side], axis=1), tab("fyb")
+        )
+        n = x1.shape[0] // count
         stacked = [
-            jnp.concatenate(
-                [x1[k * lx : (k + 1) * lx, :LANES], x1[k * lx : (k + 1) * lx, LANES:]], axis=0
-            )
-            for k in range(2)
+            jnp.concatenate([x1[k * n : (k + 1) * n, :LANES], x1[k * n : (k + 1) * n, LANES:]], 0)
+            for k in range(count)
         ]
-        hi, lo = split(jnp.concatenate(stacked, axis=1))
-        both = dot(tab("fx2"), hi)
-        x2 = both[: 2 * lx] + both[2 * lx :] + dot(tab("fx2", 0, 2 * lx), lo)
-        for k in range(2):
-            part = x2[:, k * LANES : (k + 1) * LANES]
-            own[phase, 2 * q + k, pl.ds(0, lp), :] = fold(part[:lx])
-            own[phase, 2 * q + k, pl.ds(lp, lp), :] = fold(part[lx:])
+        return [split(jnp.concatenate(stacked[k : k + 2], axis=1)) for k in range(0, count, 2)]
+
+    def forward(phase, field, planes):
+        spectra = along_y(
+            [[field[z]] for z in planes], [[beside(phase, z, EDGE, nx)] for z in planes]
+        )
+        for q, (hi, lo) in enumerate(spectra):
+            x2 = dot(tab("fxa"), jnp.concatenate([hi, lo], axis=0)) + dot(tab("fxb"), hi)
+            for k in range(2):
+                z = planes[2 * q + k]
+                part = x2[:, k * LANES : (k + 1) * LANES]
+                mix[z] = part
+
+    def forward_edges(phase, planes):
+        spectra = along_y(
+            [[xhalo[phase, side, z] for side in range(2)] for z in planes],
+            [[beside(phase, z, first, EDGE) for first in (0, EDGE + nx)] for z in planes],
+        )
+        for q, (hi, lo) in enumerate(spectra):
+            x2 = dot(tab("fxh"), jnp.concatenate([hi, lo, hi], axis=0))
+            for k in range(2):
+                z = planes[2 * q + k]
+                part = mix[z] + x2[:, k * LANES : (k + 1) * LANES]
+                own[phase, z, pl.ds(0, lp), :] = fold(part[:lx])
+                own[phase, z, pl.ds(lp, lp), :] = fold(part[lx:])
 
     def mix_planes(source, phase, base, conj, add, chosen):
         @pl.loop(0, lp // 8)
@@ -346,7 +391,8 @@
                 mix[i, im, :] = mix[i, im, :] + yi if add else yi
 
     def inverse(planes, write):
-        for z in planes:
+        rows = []
+        for z in planes[::2]:
             y = jnp.concatenate(
                 [
                     jnp.concatenate([unfold(mix[w, pl.ds(0, lp)]), unfold(mix[w, pl.ds(lp, lp)])], 0)
@@ -359,9 +405,12 @@
             g = both[: 2 * nx] + both[2 * nx :] + dot(tab("ix2", 0, 2 * nx), lo)
             for k in range(2):
                 part = g[:, k * LANES : (k + 1) * LANES]
-                rows = jnp.concatenate([part[:nx], part[nx:]], axis=1)
-                hi, lo = split(rows)
-                write(z + k, dot(hi, tab("iyh")) + dot(lo, tab("iyh")) + dot(hi, tab("iyl")))
+                rows.append(jnp.concatenate([part[:nx], part[nx:]], axis=1))
+        hi, lo = split(jnp.concatenate(rows, axis=0))
+        both = dot(hi, tab("iy2"))
+        field = both[:, :ny] + both[:, ny:] + dot(lo, tab("iy1"))
+        for k, z in enumerate(planes):
+            write(z, field[k * nx : (k + 1) * nx])
 
     def prepare(first):
         block = psf_pad[pl.ds(first, GROUP)].reshape(GROUP * wide, LANES)
@@ -389,14 +438,17 @@
                 k2[first + 2 * h + n, pl.ds(lp, lp), :] = fold(part[lx:])
 
     def convolve(phase, field, conj, groups, write, after):
-        with NS(f"wait_halo{phase}"):
-            settle(hr.at[phase])
-        count = nz // 2
-        for n in range(2):
-            with NS(f"forward{phase}_{n}"):
-                for q in range(n * pairs // 2, (n + 1) * pairs // 2):
-                    forward(phase, field, q)
-                swap_copy(phase, n * count, count).start()
+        with NS(f"wait_haloy{phase}"):
+            settle(hy.at[phase], along_x=False)
+        with NS(f"forward{phase}"):
+            for z in range(0, nz, 8):
+                forward(phase, field, range(z, z + 8))
+        with NS(f"wait_halox{phase}"):
+            settle(hx.at[phase], along_y=False)
+        with NS(f"edges{phase}"):
+            for first, count in ((0, 8),):
+                forward_edges(phase, range(first, first + count))
+                swap_copy(phase, first, count).start()
         sign = 1 - 2 * gz if conj else 2 * gz - 1
         with NS(f"mixown{phase}"):
             mix_planes(own, phase, middle, conj, False, range(nz))
@@ -405,13 +457,13 @@
                 prepare(3 * GROUP * gz)
         with NS(f"waitswap{phase}"):
             pltpu.make_async_copy(own.at[phase], peer.at[phase], er.at[phase]).wait()
+        with NS(f"mixpeer{phase}"):
+            mix_planes(peer, phase, middle + sign * nz, conj, True, range(nz))
         size = nz // groups
         for n in range(groups):
             planes = range(n * size, (n + 1) * size)
-            with NS(f"mixpeer{phase}_{n}"):
-                mix_planes(peer, phase, middle + sign * nz, conj, True, planes)
             with NS(f"inverse{phase}_{n}"):
-                inverse(planes[::2], write)
+                inverse(planes, write)
                 after(planes)
 
     with NS("zero"):
@@ -420,14 +472,13 @@
     with NS("wait_est"):
         load_est.wait()
     with NS("pack0"):
-        for z in range(nz):
-            add_to_pack(0, z, est_ref[z], z == 0)
+        add_to_pack(0, est_ref, range(nz))
     with NS("barrier"):
         pl.semaphore_wait(barrier, everyone - 1)
     with NS("send0"):
+        send_halo(0, est_ref, SIDES_Y)
         send_halo(0, est_ref, CORNERS)
         send_halo(0, est_ref, SIDES_X, pl.ds(0, nz))
-        send_halo(0, est_ref, SIDES_Y)
 
     with NS("wait_loads"):
         load_index.wait()
@@ -450,16 +501,15 @@
             prepare(g * GROUP)
 
     def write_ratio(z, blurred):
-        value = view_ref[z] / blurred
-        ratio[z] = value
-        add_to_pack(1, z, value, z == 0)
+        ratio[z] = view_ref[z] / blurred
 
     def after_ratio(planes):
+        add_to_pack(1, ratio, planes)
+        if planes[-1] == nz - 1:
+            send_halo(1, ratio, SIDES_Y)
         if planes[-1] == nz - 1:
             send_halo(1, ratio, CORNERS)
         send_halo(1, ratio, SIDES_X, pl.ds(planes[0], len(planes)))
-        if planes[-1] == nz - 1:
-            send_halo(1, ratio, SIDES_Y)
 
     convolve(0, est_ref, False, 2, write_ratio, after_ratio)
 
@@ -488,20 +538,17 @@
         def slot(x, y, z):
             return (x * gyn + y) * 2 + z
 
-        def tile_copy(offset):
-            return pltpu.make_async_remote_copy(
+        def send_tile(device):
+            pltpu.make_async_remote_copy(
                 src_ref=mine,
                 dst_ref=tiles.at[slot(gx, gy, gz)],
                 send_sem=gs,
                 recv_sem=gr,
-                device_id=device_at(offset),
+                device_id=device,
                 device_id_type=MESH,
-            )
-
-        @pl.loop(1, everyone)
-        def _(offset):
-            tile_copy(offset).start()
-
+            ).start()
+
+        for_others(send_tile)
         tiles[slot(gx, gy, gz)] = mine[...]
 
     def pooled(plane):
@@ -595,7 +642,7 @@
             pltpu.VMEM((wide, 2 * lp, LANES), F32),
             pltpu.VMEM((2, nz, 2 * lp, LANES), F32),
             pltpu.VMEM((2, nz, 2 * lp, LANES), F32),
-            pltpu.VMEM((nz, 2 * lp, LANES), F32),
+            pltpu.VMEM((nz, 2 * lx, LANES), F32),
             pltpu.VMEM((nz, nx, ny), F32),
             pltpu.VMEM((2, 2, nx, LANES), F32),
             pltpu.VMEM((2, 2, nz, EDGE, ny), F32),
@@ -607,6 +654,7 @@
             pltpu.VMEM((everyone, rows5, LANES), F32),
             pltpu.VMEM((2 * nz * EDGE + 2 * nx + 4 * EDGE, LANES), F32),
             dma((5,)),
+            dma((2,)),
             dma((2,)),
             dma((2,)),
             dma((2,)),

time: 33.3 us -> 30 us (0.901)
  Pallas kernels: 31.9 us -> 28.6 us
    pallas_call x1, Pallas kernels: 31.1 us -> 27.8 us  [local(): pl.pallas_call(functools.partial(kernel, sizes, where, places), out_shape...]
where the time goes in v2:
time: 30 us; the launch traced here: 29.9 us
  Pallas kernels  28.6 us (95%)
  between operations  1.29 us (4%)
    pallas_call x1, Pallas kernels, local(): pl.pallas_call(functools.partial(kernel, sizes, where, places), out_shape...  27.8 us
    pallas_call x1, Pallas kernels, local(): pl.pallas_call(write_out, out_shape=tuple((jax.ShapeDtypeStruct(s, F32) f...  0.78 us

profile of v2, /device:TPU:0, one launch (start us, length us, event | category | flops | bytes accessed | tf_op | source)
XLA Modules:
  0.0 29.9 jit_solution(8365848020471198472)
XLA Ops:
  1.3 27.8 %deconvolve.1 = (f32[8,64,128]{2,1,0:T(8,128)S(1)}, f32[4,32,64]{2,1,0:T(8,128)S(1)}, f32[2,16,32]{2,1,0:T(8,128)S(1)}, f32[1,8,16]{2,1,0:T(8,128)S(1)}, f32[1,4...) custom-call(s32[1]{0:T(128)S(6)} %copy.11.index_hbm, f32[8,64,128]{2,1,0:T(8,128)} %est_hbm.1, f32[8,64,128]{2,1,0:T(8,128)} %view_hbm.1, ...), custom_call_target="tpu_custom_call" | custom-call | tf_op jit(solution)/shard_map/deconvolve/pallas_call | solution.py:630
  29.1 0.8 %write_out.1 = (f32[8,64,128]{2,1,0:T(8,128)}, f32[4,32,64]{2,1,0:T(8,128)}, f32[2,16,32]{2,1,0:T(8,128)}, f32[1,8,16]{2,1,0:T(8,128)}, f32[1,4,8]{2,1,0:T(4,128)}, /*index=5*/f32[1,8,16]{2,1,0:T(8,128)}) custom-call(f32[8,64,128]{2,1,0:T(8,128)S(1)} %get-tuple-element.12.refs_0_, f32[4,32,64]{2,1,0:T(8,128)S(1)} %get-tuple-element.13.refs_1_, ...), custom_call_target="tpu_custom_call" | custom-call | tf_op jit(solution)/shard_map/write_out/pallas_call | solution.py:678

commit v3 on v2

--- a/solution.py
+++ b/solution.py
@@ -16,6 +16,8 @@
 LANES = 128
 EDGE = 16
 GROUP = 8
+CHUNKS = 4
+STEPS = ((0, 8),)
 CORNERS = ((1, 1), (-1, 1), (1, -1), (-1, -1))
 SIDES_X = ((1, 0), (-1, 0))
 SIDES_Y = ((0, 1), (0, -1))
@@ -99,6 +101,9 @@
 
     inner = np.concatenate([EDGE + np.arange(nx), lx + EDGE + np.arange(nx)])
     outer = np.setdiff1d(np.arange(2 * lx), inner)
+    x_edge = np.concatenate([np.arange(EDGE), nx - EDGE + np.arange(EDGE)])
+    x_middle = EDGE + np.arange(nx - 2 * EDGE)
+    inverse_rows = np.concatenate([x_edge, nx + x_edge, x_middle, nx + x_middle])
     blank = np.zeros((LANES - 3 * wide, 2 * LANES), BF)
     side_hi, side_lo = fy_hi[ny:], fy_lo[ny:]
     named = {
@@ -109,7 +114,7 @@
         "fxh": np.concatenate([fx_hi[:, outer], fx_hi[:, outer], fx_lo[:, outer]], 1),
         "ky3": np.concatenate([ky_hi, ky_hi, ky_lo, blank], 0),
         "kx3": np.concatenate([kx_hi, kx_hi, kx_lo], 1),
-        "ix2": np.concatenate([ix_hi, ix_lo], 0),
+        "ix2": np.concatenate([part[inverse_rows] for part in (ix_hi, ix_lo)], 0),
         "iy2": np.concatenate([iy_hi, iy_lo], 1),
         "iy1": iy_hi,
         "py": py.astype(BF),
@@ -131,7 +136,7 @@
     index_hbm, est_hbm, view_hbm, psf_hbm, table_hbm,
     out_ref, one_ref, two_ref, three_ref, four_ref, five_ref,
     index_ref, est_ref, view_ref, psf, table,
-    psf_pad, k2, own, peer, mix, ratio,
+    psf_pad, k2, own, peer, mix, parts_of, ratio,
     pack, xhalo, yhalo, share, share_in, place5, mine, tiles, ruler,
     in_sem, hs, hx, hy, es, er, ps, pr, gs, gr,
 ):
@@ -194,13 +199,6 @@
     def signal(device):
         pl.semaphore_signal(barrier, inc=1, device_id=device, device_id_type=MESH)
 
-    barrier = pltpu.get_barrier_semaphore()
-    for_others(signal)
-    load_psf.start()
-    load_index.start()
-    load_table.start()
-    load_view.start()
-
     def exists(dx, dy):
         ok = None
         for c, n, d in ((gx, gxn, dx), (gy, gyn, dy)):
@@ -212,6 +210,25 @@
                 continue
             ok = t if ok is None else jnp.logical_and(ok, t)
         return ok
+
+    beside_x = (gx > 0).astype(jnp.int32) + (gx < gxn - 1).astype(jnp.int32)
+    beside_y = (gy > 0).astype(jnp.int32) + (gy < gyn - 1).astype(jnp.int32)
+
+    barrier = pltpu.get_barrier_semaphore()
+    close = max(gxn, gyn) <= 4
+    if close:
+        signal(partner)
+        for dx, dy in SIDES_X + SIDES_Y + CORNERS:
+
+            @pl.when(exists(dx, dy))
+            def _():
+                signal({"gx": gx + dx, "gy": gy + dy, "gz": gz})
+    else:
+        for_others(signal)
+    load_psf.start()
+    load_index.start()
+    load_table.start()
+    load_view.start()
 
     def halo_copy(phase, field, dx, dy, planes=None):
         if dy == 0:
@@ -251,9 +268,6 @@
             else:
                 send(dx, dy)
 
-    beside_x = (gx > 0).astype(jnp.int32) + (gx < gxn - 1).astype(jnp.int32)
-    beside_y = (gy > 0).astype(jnp.int32) + (gy < gyn - 1).astype(jnp.int32)
-
     def settle(sem, along_x=True, along_y=True):
         for a in range(3):
             for b in range(3):
@@ -265,15 +279,16 @@
                         part = ruler.at[pl.ds(0, rows)]
                         pltpu.make_async_copy(part, part, sem).wait()
 
-    def add_to_pack(phase, field, planes):
-        lane = lax.broadcasted_iota(jnp.int32, (nx, LANES), 1) // EDGE
+    def do_pack(phase, field, rows):
+        count = rows.size
+        lane = lax.broadcasted_iota(jnp.int32, (count, LANES), 1) // EDGE
         for side in range(2):
-            kept = pack[phase, side] if planes[0] else jnp.zeros((nx, LANES), F32)
-            for z in planes:
+            packed = jnp.zeros((count, LANES), F32)
+            for z in range(nz):
                 shift = (EDGE * z + EDGE * (1 - side)) % LANES
-                moved = pltpu.roll(field[z], shift, 1) if shift else field[z]
-                kept = jnp.where(lane == z, moved, kept)
-            pack[phase, side] = kept
+                cells = field[z, rows, :]
+                packed = jnp.where(lane == z, pltpu.roll(cells, shift, 1) if shift else cells, packed)
+            pack[phase, side, rows, :] = packed
 
     def zero_missing(phase):
         for dx, dy in SIDES_X + SIDES_Y + CORNERS:
@@ -288,13 +303,13 @@
             def _():
                 target[...] = jnp.zeros(target.shape, F32)
 
-    def swap_copy(phase, first, count):
-        planes = pl.ds(first, count)
+    def swap_copy(phase, n):
+        planes = pl.ds(n * nz // CHUNKS, nz // CHUNKS)
         return pltpu.make_async_remote_copy(
             src_ref=own.at[phase, planes],
             dst_ref=peer.at[phase, planes],
             send_sem=es.at[phase],
-            recv_sem=er.at[phase],
+            recv_sem=er.at[phase, n],
             device_id=partner,
             device_id_type=MESH,
         )
@@ -363,23 +378,22 @@
                 own[phase, z, pl.ds(0, lp), :] = fold(part[:lx])
                 own[phase, z, pl.ds(lp, lp), :] = fold(part[lx:])
 
-    def mix_planes(source, phase, base, conj, add, chosen):
+    def mix_planes(source, phase, base, conj, add, taken):
         @pl.loop(0, lp // 8)
         def _(s):
             re = pl.ds(pl.multiple_of(s * 8, 8), 8)
             im = pl.ds(pl.multiple_of(lp + s * 8, 8), 8)
-            vr = [source[phase, j, re, :] for j in range(nz)]
-            vi = [source[phase, j, im, :] for j in range(nz)]
+            vr = {j: source[phase, j, re, :] for j in taken}
+            vi = {j: source[phase, j, im, :] for j in taken}
             kr, ki = {}, {}
-            reach = [(j - i if conj else i - j) for i in chosen for j in range(nz)]
-            for d in sorted(set(reach)):
+            for d in sorted({j - i if conj else i - j for i in range(nz) for j in taken}):
                 kr[d] = k2[base + d, re, :]
                 ki[d] = k2[base + d, im, :]
             ks = {d: kr[d] - ki[d] if conj else kr[d] + ki[d] for d in kr}
-            vs = [r + i for r, i in zip(vr, vi)]
-            for i in chosen:
+            vs = {j: vr[j] + vi[j] for j in taken}
+            for i in range(nz):
                 a = b = c = None
-                for j in range(nz):
+                for j in taken:
                     d = j - i if conj else i - j
                     rr, ii, ss = kr[d] * vr[j], ki[d] * vi[j], ks[d] * vs[j]
                     a = rr if a is None else a + rr
@@ -390,27 +404,39 @@
                 mix[i, re, :] = mix[i, re, :] + yr if add else yr
                 mix[i, im, :] = mix[i, im, :] + yi if add else yi
 
-    def inverse(planes, write):
+    segments = (((0, EDGE), (nx - EDGE, EDGE)), ((EDGE, nx - 2 * EDGE),))
+
+    def unfolded(z):
+        return jnp.concatenate([unfold(mix[z, pl.ds(0, lp)]), unfold(mix[z, pl.ds(lp, lp)])], 0)
+
+    def inverse(planes, parts, write, keep=False, kept=False):
+        counts = [sum(count for _, count in segments[p]) for p in parts]
+        offset = 2 * sum(count for _, count in segments[0]) * parts[0]
         rows = []
         for z in planes[::2]:
-            y = jnp.concatenate(
-                [
-                    jnp.concatenate([unfold(mix[w, pl.ds(0, lp)]), unfold(mix[w, pl.ds(lp, lp)])], 0)
-                    for w in (z, z + 1)
-                ],
-                axis=1,
-            )
-            hi, lo = split(y)
-            both = dot(tab("ix2"), hi)
-            g = both[: 2 * nx] + both[2 * nx :] + dot(tab("ix2", 0, 2 * nx), lo)
+            if kept:
+                hi, lo = parts_of[z // 2, 0], parts_of[z // 2, 1]
+            else:
+                hi, lo = split(jnp.concatenate([unfolded(z), unfolded(z + 1)], axis=1))
+            if keep:
+                parts_of[z // 2, 0] = hi
+                parts_of[z // 2, 1] = lo
+            high = tab("ix2", offset, 2 * sum(counts))
+            g = dot(high, hi) + dot(tab("ix2", 2 * nx + offset, 2 * sum(counts)), hi) + dot(high, lo)
             for k in range(2):
                 part = g[:, k * LANES : (k + 1) * LANES]
-                rows.append(jnp.concatenate([part[:nx], part[nx:]], axis=1))
+                for count in counts:
+                    rows.append(jnp.concatenate([part[:count], part[count : 2 * count]], axis=1))
+                    part = part[2 * count :]
         hi, lo = split(jnp.concatenate(rows, axis=0))
         both = dot(hi, tab("iy2"))
-        field = both[:, :ny] + both[:, ny:] + dot(lo, tab("iy1"))
-        for k, z in enumerate(planes):
-            write(z, field[k * nx : (k + 1) * nx])
+        values = both[:, :ny] + both[:, ny:] + dot(lo, tab("iy1"))
+        row = 0
+        for z in planes:
+            for p in parts:
+                for first, count in segments[p]:
+                    write(z, pl.ds(first, count), values[row : row + count])
+                    row += count
 
     def prepare(first):
         block = psf_pad[pl.ds(first, GROUP)].reshape(GROUP * wide, LANES)
@@ -437,34 +463,31 @@
                 k2[first + 2 * h + n, pl.ds(0, lp), :] = fold(part[:lx])
                 k2[first + 2 * h + n, pl.ds(lp, lp), :] = fold(part[lx:])
 
-    def convolve(phase, field, conj, groups, write, after):
+    def convolve(phase, field, conj, invert):
         with NS(f"wait_haloy{phase}"):
             settle(hy.at[phase], along_x=False)
         with NS(f"forward{phase}"):
             for z in range(0, nz, 8):
                 forward(phase, field, range(z, z + 8))
+        if phase == 0:
+            with NS("prepare2"):
+                prepare(3 * GROUP * gz)
         with NS(f"wait_halox{phase}"):
             settle(hx.at[phase], along_y=False)
         with NS(f"edges{phase}"):
-            for first, count in ((0, 8),):
-                forward_edges(phase, range(first, first + count))
-                swap_copy(phase, first, count).start()
+            forward_edges(phase, range(nz))
+            for n in range(CHUNKS):
+                swap_copy(phase, n).start()
         sign = 1 - 2 * gz if conj else 2 * gz - 1
         with NS(f"mixown{phase}"):
             mix_planes(own, phase, middle, conj, False, range(nz))
-        if phase == 0:
-            with NS("prepare2"):
-                prepare(3 * GROUP * gz)
-        with NS(f"waitswap{phase}"):
-            pltpu.make_async_copy(own.at[phase], peer.at[phase], er.at[phase]).wait()
-        with NS(f"mixpeer{phase}"):
-            mix_planes(peer, phase, middle + sign * nz, conj, True, range(nz))
-        size = nz // groups
-        for n in range(groups):
-            planes = range(n * size, (n + 1) * size)
-            with NS(f"inverse{phase}_{n}"):
-                inverse(planes, write)
-                after(planes)
+        for n in range(CHUNKS):
+            with NS(f"waitswap{phase}_{n}"):
+                swap_copy(phase, n).wait_recv()
+            with NS(f"mixpeer{phase}_{n}"):
+                taken = range(n * nz // CHUNKS, (n + 1) * nz // CHUNKS)
+                mix_planes(peer, phase, middle + sign * nz, conj, True, taken)
+        invert()
 
     with NS("zero"):
         zero_missing(0)
@@ -472,9 +495,12 @@
     with NS("wait_est"):
         load_est.wait()
     with NS("pack0"):
-        add_to_pack(0, est_ref, range(nz))
+        do_pack(0, est_ref, pl.ds(0, nx))
     with NS("barrier"):
-        pl.semaphore_wait(barrier, everyone - 1)
+        if close:
+            pl.semaphore_wait(barrier, beside_x + beside_y + beside_x * beside_y + 1)
+        else:
+            pl.semaphore_wait(barrier, everyone - 1)
     with NS("send0"):
         send_halo(0, est_ref, SIDES_Y)
         send_halo(0, est_ref, CORNERS)
@@ -500,18 +526,33 @@
         def _(g):
             prepare(g * GROUP)
 
-    def write_ratio(z, blurred):
-        ratio[z] = view_ref[z] / blurred
-
-    def after_ratio(planes):
-        add_to_pack(1, ratio, planes)
-        if planes[-1] == nz - 1:
+    def write_ratio(z, rows, blurred):
+        ratio[z, rows, :] = view_ref[z, rows, :] / blurred
+
+    def invert_blurred():
+        for first, count in STEPS:
+            with NS(f"inverse0_{first}"):
+                inverse(range(first, first + count), (0,), write_ratio, keep=True)
+                if first + count == nz:
+                    for start, rows in segments[0]:
+                        do_pack(1, ratio, pl.ds(start, rows))
+                    send_halo(1, ratio, CORNERS)
+
+                @pl.when(gz == 0)
+                def _():
+                    send_halo(1, ratio, SIDES_X, pl.ds(first, count))
+
+        with NS("inverse0_middle"):
+            inverse(range(nz), (1,), write_ratio, kept=True)
+            @pl.when(gz == 1)
+            def _():
+                send_halo(1, ratio, SIDES_X, pl.ds(0, nz))
+
+            for start, rows in segments[1]:
+                do_pack(1, ratio, pl.ds(start, rows))
             send_halo(1, ratio, SIDES_Y)
-        if planes[-1] == nz - 1:
-            send_halo(1, ratio, CORNERS)
-        send_halo(1, ratio, SIDES_X, pl.ds(planes[0], len(planes)))
-
-    convolve(0, est_ref, False, 2, write_ratio, after_ratio)
+
+    convolve(0, est_ref, False, invert_blurred)
 
     with NS("prepare3"):
         prepare(3 * GROUP * (1 - gz))
@@ -521,10 +562,14 @@
         target = i // (ny // cols5) + gy * cols5
         place5[...] = jnp.where(j == target, 1.0 / (nz * 2 * 32 * 32), 0.0).astype(BF)
 
-    def write_update(z, correction):
-        out_ref[z] = est_ref[z] * correction
-
-    convolve(1, ratio, True, 1, write_update, lambda planes: None)
+    def write_update(z, rows, correction):
+        out_ref[z, rows, :] = est_ref[z, rows, :] * correction
+
+    def invert_correction():
+        with NS("inverse1"):
+            inverse(range(nz), (0, 1), write_update)
+
+    convolve(1, ratio, True, invert_correction)
 
     with NS("five_send"):
         rows5 = four_ref.shape[1] // 2
@@ -643,6 +688,7 @@
             pltpu.VMEM((2, nz, 2 * lp, LANES), F32),
             pltpu.VMEM((2, nz, 2 * lp, LANES), F32),
             pltpu.VMEM((nz, 2 * lx, LANES), F32),
+            pltpu.VMEM((nz // 2, 2, 2 * lx, 2 * LANES), BF),
             pltpu.VMEM((nz, nx, ny), F32),
             pltpu.VMEM((2, 2, nx, LANES), F32),
             pltpu.VMEM((2, 2, nz, EDGE, ny), F32),
@@ -658,7 +704,7 @@
             dma((2,)),
             dma((2,)),
             dma((2,)),
-            dma((2,)),
+            dma((2, CHUNKS)),
             dma,
             dma,
             dma,

time: 30 us -> 28.9 us (0.963)
  Pallas kernels: 28.6 us -> 27.5 us
    pallas_call x1, Pallas kernels: 27.8 us -> 26.7 us  [local(): pl.pallas_call(functools.partial(kernel, sizes, where, places), out_shape...]
where the time goes in v3:
time: 28.9 us; the launch traced here: 28.7 us
  Pallas kernels  27.5 us (95%)
  between operations  1.29 us (4%)
    pallas_call x1, Pallas kernels, local(): pl.pallas_call(functools.partial(kernel, sizes, where, places), out_shape...  26.7 us
    pallas_call x1, Pallas kernels, local(): pl.pallas_call(write_out, out_shape=tuple((jax.ShapeDtypeStruct(s, F32) f...  0.78 us

profile of v3, /device:TPU:0, one launch (start us, length us, event | category | flops | bytes accessed | tf_op | source)
XLA Modules:
  0.0 28.7 jit_solution(16180375121902658454)
XLA Ops:
  1.3 26.7 %deconvolve.1 = (f32[8,64,128]{2,1,0:T(8,128)S(1)}, f32[4,32,64]{2,1,0:T(8,128)S(1)}, f32[2,16,32]{2,1,0:T(8,128)S(1)}, f32[1,8,16]{2,1,0:T(8,128)S(1)}, f32[1,4...) custom-call(s32[1]{0:T(128)S(6)} %copy.11.index_hbm, f32[8,64,128]{2,1,0:T(8,128)} %est_hbm.1, f32[8,64,128]{2,1,0:T(8,128)} %view_hbm.1, ...), custom_call_target="tpu_custom_call" | custom-call | tf_op jit(solution)/shard_map/deconvolve/pallas_call | solution.py:675
  28.0 0.8 %write_out.1 = (f32[8,64,128]{2,1,0:T(8,128)}, f32[4,32,64]{2,1,0:T(8,128)}, f32[2,16,32]{2,1,0:T(8,128)}, f32[1,8,16]{2,1,0:T(8,128)}, f32[1,4,8]{2,1,0:T(4,128)}, /*index=5*/f32[1,8,16]{2,1,0:T(8,128)}) custom-call(f32[8,64,128]{2,1,0:T(8,128)S(1)} %get-tuple-element.12.refs_0_, f32[4,32,64]{2,1,0:T(8,128)S(1)} %get-tuple-element.13.refs_1_, ...), custom_call_target="tpu_custom_call" | custom-call | tf_op jit(solution)/shard_map/write_out/pallas_call | solution.py:724

commit v4 on v3

--- a/solution.py
+++ b/solution.py
@@ -16,8 +16,8 @@
 LANES = 128
 EDGE = 16
 GROUP = 8
-CHUNKS = 4
-STEPS = ((0, 8),)
+CHUNKS = 2
+STEPS = ((0, 4), (4, 4))
 CORNERS = ((1, 1), (-1, 1), (1, -1), (-1, -1))
 SIDES_X = ((1, 0), (-1, 0))
 SIDES_Y = ((0, 1), (0, -1))
@@ -183,7 +183,7 @@
                     if not (skip and b == 0 and c == 0):
                         act({"gx": x, "gy": y, "gz": zs[c]})
 
-        order = sorted(range(gyn), key=lambda b: -min(b, gyn - b))
+        order = (*range(1, gyn), 0)
         ys = [(b, lax.rem(gy + b, gyn)) for b in order]
         if gxn <= 4:
             for a in (*range(1, gxn), 0):
@@ -542,11 +542,17 @@
                 def _():
                     send_halo(1, ratio, SIDES_X, pl.ds(first, count))
 
+                if first:
+
+                    @pl.when(gz == 1)
+                    def _():
+                        send_halo(1, ratio, SIDES_X, pl.ds(0, first))
+
         with NS("inverse0_middle"):
             inverse(range(nz), (1,), write_ratio, kept=True)
             @pl.when(gz == 1)
             def _():
-                send_halo(1, ratio, SIDES_X, pl.ds(0, nz))
+                send_halo(1, ratio, SIDES_X, pl.ds(*STEPS[-1]))
 
             for start, rows in segments[1]:
                 do_pack(1, ratio, pl.ds(start, rows))

time: 28.9 us -> 28.5 us (0.986)
  Pallas kernels: 27.5 us -> 27 us
    pallas_call x1, Pallas kernels: 26.7 us -> 26.3 us  [local(): pl.pallas_call(functools.partial(kernel, sizes, where, places), out_shape...]
where the time goes in v4:
time: 28.5 us; the launch traced here: 28.3 us
  Pallas kernels  27 us (95%)
  between operations  1.29 us (5%)
    pallas_call x1, Pallas kernels, local(): pl.pallas_call(functools.partial(kernel, sizes, where, places), out_shape...  26.3 us
    pallas_call x1, Pallas kernels, local(): pl.pallas_call(write_out, out_shape=tuple((jax.ShapeDtypeStruct(s, F32) f...  0.78 us

profile of v4, /device:TPU:0, one launch (start us, length us, event | category | flops | bytes accessed | tf_op | source)
XLA Modules:
  0.0 28.3 jit_solution(948125056178204380)
XLA Ops:
  1.3 26.3 %deconvolve.1 = (f32[8,64,128]{2,1,0:T(8,128)S(1)}, f32[4,32,64]{2,1,0:T(8,128)S(1)}, f32[2,16,32]{2,1,0:T(8,128)S(1)}, f32[1,8,16]{2,1,0:T(8,128)S(1)}, f32[1,4...) custom-call(s32[1]{0:T(128)S(6)} %copy.11.index_hbm, f32[8,64,128]{2,1,0:T(8,128)} %est_hbm.1, f32[8,64,128]{2,1,0:T(8,128)} %view_hbm.1, ...), custom_call_target="tpu_custom_call" | custom-call | tf_op jit(solution)/shard_map/deconvolve/pallas_call | solution.py:681
  27.6 0.8 %write_out.1 = (f32[8,64,128]{2,1,0:T(8,128)}, f32[4,32,64]{2,1,0:T(8,128)}, f32[2,16,32]{2,1,0:T(8,128)}, f32[1,8,16]{2,1,0:T(8,128)}, f32[1,4,8]{2,1,0:T(4,128)}, /*index=5*/f32[1,8,16]{2,1,0:T(8,128)}) custom-call(f32[8,64,128]{2,1,0:T(8,128)S(1)} %get-tuple-element.12.refs_0_, f32[4,32,64]{2,1,0:T(8,128)S(1)} %get-tuple-element.13.refs_1_, ...), custom_call_target="tpu_custom_call" | custom-call | tf_op jit(solution)/shard_map/write_out/pallas_call | solution.py:730

commit v5 on v4

--- a/solution.py
+++ b/solution.py
@@ -379,7 +379,7 @@
                 own[phase, z, pl.ds(lp, lp), :] = fold(part[lx:])
 
     def mix_planes(source, phase, base, conj, add, taken):
-        @pl.loop(0, lp // 8)
+        @pl.loop(0, lp // 8, unroll=2)
         def _(s):
             re = pl.ds(pl.multiple_of(s * 8, 8), 8)
             im = pl.ds(pl.multiple_of(lp + s * 8, 8), 8)

time: 28.5 us -> 28.3 us (level)
  no operation moved by 1% of the time
where the time goes in v5:
time: 28.3 us; the launch traced here: 28.2 us
  Pallas kernels  26.9 us (95%)
  between operations  1.29 us (5%)
    pallas_call x1, Pallas kernels, local(): pl.pallas_call(functools.partial(kernel, sizes, where, places), out_shape...  26.1 us
    pallas_call x1, Pallas kernels, local(): pl.pallas_call(write_out, out_shape=tuple((jax.ShapeDtypeStruct(s, F32) f...  0.78 us

profile of v5, /device:TPU:0, one launch (start us, length us, event | category | flops | bytes accessed | tf_op | source)
XLA Modules:
  0.0 28.2 jit_solution(12550485476323671654)
XLA Ops:
  1.3 26.1 %deconvolve.1 = (f32[8,64,128]{2,1,0:T(8,128)S(1)}, f32[4,32,64]{2,1,0:T(8,128)S(1)}, f32[2,16,32]{2,1,0:T(8,128)S(1)}, f32[1,8,16]{2,1,0:T(8,128)S(1)}, f32[1,4...) custom-call(s32[1]{0:T(128)S(6)} %copy.11.index_hbm, f32[8,64,128]{2,1,0:T(8,128)} %est_hbm.1, f32[8,64,128]{2,1,0:T(8,128)} %view_hbm.1, ...), custom_call_target="tpu_custom_call" | custom-call | tf_op jit(solution)/shard_map/deconvolve/pallas_call | solution.py:681
  27.4 0.8 %write_out.1 = (f32[8,64,128]{2,1,0:T(8,128)}, f32[4,32,64]{2,1,0:T(8,128)}, f32[2,16,32]{2,1,0:T(8,128)}, f32[1,8,16]{2,1,0:T(8,128)}, f32[1,4,8]{2,1,0:T(4,128)}, /*index=5*/f32[1,8,16]{2,1,0:T(8,128)}) custom-call(f32[8,64,128]{2,1,0:T(8,128)S(1)} %get-tuple-element.12.refs_0_, f32[4,32,64]{2,1,0:T(8,128)S(1)} %get-tuple-element.13.refs_1_, ...), custom_call_target="tpu_custom_call" | custom-call | tf_op jit(solution)/shard_map/write_out/pallas_call | solution.py:730
